TPU v7x, 32 devices: a whole 2x2x4 slice. The times are simulated.
32 devices in a mesh: dp: 8 (over z, x), col: 4 (over y, core).
Axes of the slice: x: 2, y: 2, z: 4, core: 2. Of those that a mesh axis runs over, the one named last changes fastest.
Arguments:
- tokens: bfloat16 [50432, 384], P(('dp', 'col')), may hold values from -40 to 40
- packed: bfloat16 [384, 1152], P('dp', 'col'), may hold values from -0.3125 to 0.3125
- packed_bias: float32 [1152], P('col'), may hold values from -3 to 3
- projection: bfloat16 [384, 384], P('col', 'dp'), may hold values from -2.5 to 2.5
- projection_bias: float32 [384], replicated, may hold values from -3 to 3
- expansion: bfloat16 [384, 1536], P('dp', 'col'), may hold values from -0.3125 to 0.3125
- expansion_bias: float32 [1536], P('col'), may hold values from -3 to 3
- reduction: bfloat16 [1536, 384], P('col', 'dp'), may hold values from -0.15625 to 0.15625
- reduction_bias: float32 [384], replicated, may hold values from -3 to 3
- first_scale: float32 [384], replicated, may hold values from 0.25 to 1.75
- first_shift: float32 [384], replicated, may hold values from -3 to 3
- second_scale: float32 [384], replicated, may hold values from 0.25 to 1.75
- second_shift: float32 [384], replicated, may hold values from -3 to 3
- upstream: bfloat16 [50432, 384], P(('dp', 'col')), may hold values from -6 to 6
Outputs:
- layer_output: bfloat16 [50432, 384], P(('dp', 'col'))
- input_grad: float32 [50432, 384], P(('dp', 'col'))
- packed_grad: float32 [384, 1152], P('dp', 'col')
- projection_grad: float32 [384, 384], P('col', 'dp')
- expansion_grad: float32 [384, 1536], P('dp', 'col')
- reduction_grad: float32 [1536, 384], P('col', 'dp')
- packed_bias_grad: float32 [1152], P('col')
- projection_bias_grad: float32 [384], P('col')
- expansion_bias_grad: float32 [1536], P('col')
- reduction_bias_grad: float32 [384], P('col')
- first_scale_grad: float32 [384], P('col')
- first_shift_grad: float32 [384], P('col')
- second_scale_grad: float32 [384], P('col')
- second_shift_grad: float32 [384], P('col')
All inputs are finite; a program needn't handle non-finite values.
Results may differ from a plain program's by a relative error of at most 0.023.
Values may be sent and summed in bfloat16 or wider, within the bound.
A program may use at most 192 MiB of HBM per device.

v0:
```python
import functools

import jax
import jax.numpy as jnp
from jax import lax
from jax.experimental import pallas as pl
from jax.experimental.pallas import tpu as pltpu
from jax.sharding import PartitionSpec as P

SEQ = 197
EPS = 1e-06
ROOT_HALF = 0.7071067811865476
INV_ROOT_TAU = 0.3989422804014327
F32, BF16 = jnp.float32, jnp.bfloat16
MESH = pl.DeviceIdType.MESH
D = 384
FF = 1536
PAIRS = 3
WIN = 224
KEYS = 256
BIG = 528
SMALL = 176
HC = 512


def nn(a, b):
    return lax.dot_general(a, b, (((1,), (0,)), ((), ())), preferred_element_type=F32)


def nt(a, b):
    return lax.dot_general(a, b, (((1,), (1,)), ((), ())), preferred_element_type=F32)


def tn(a, b):
    return lax.dot_general(a, b, (((0,), (0,)), ((), ())), preferred_element_type=F32)


def rows_of(i, size):
    return pl.ds(pl.multiple_of(i * size, 16), size)


def lanes_of(i, size):
    return pl.ds(pl.multiple_of(i * size, 128), size)


def mean(x):
    return jnp.sum(x, axis=1, keepdims=True) * (1.0 / x.shape[1])


def hook(i, steps):
    for at, step in steps:
        pl.when(i == at)(step)


TILES = (
    ((0, 0, 128), (1, 1, 128), (2, 3, 96)),
    ((0, 0, 128), (1, 2, 64), (3, 3, 128)),
    ((0, 1, 32), (2, 2, 128), (3, 3, 128)),
)
SHARES = ((0, 1, 2, 2), (0, 1, 1, 2), (0, 0, 1, 2))


def layer_kernel(cfg, *refs):
    Z, PD, Y, RB, RV, rows = cfg
    PLANE = PD * Y
    RP = -(-rows // BIG) * BIG
    images = rows // SEQ
    nsm, nbig = RP // SMALL, RP // BIG
    (tokens, packed, packed_bias, projection, projection_bias, expansion, expansion_bias, reduction,
     reduction_bias, first_scale, first_shift, second_scale, second_shift, upstream,
     out_hbm, grad_hbm, o_packed, o_projection, o_expansion, o_reduction,
     o_pb, o_prb, o_eb, o_rb, o_fs, o_fh, o_ss, o_sh,
     x, up, n1, rows1, qkv, attn, est, rinv, n2, rows2, acc1, rg, act, hg, rgb, ag, pgr, inv1, inv2,
     wpk, ptr, exr, rtr, wp, pt, exc, rtc, bias,
     gm, gh, rm1, rm2, rm3, rh1, rh2, rh3, sm1, sm2, sh1, sh2, frame, vec, vsum1, vr1, vr2, vr3, eb,
     csem, zs, zr, ps, pr, ks, kr, bs, br, gs, gr_) = refs

    dp_i, col_i = lax.axis_index("dp"), lax.axis_index("col")
    z, pd = dp_i // PD, lax.rem(dp_i, PD)
    y, core = col_i // 2, lax.rem(col_i, 2)
    pos = core * Y + y
    plane = pd * Y + y

    def device(zz, pp, yy, cc):
        return (zz * PD + pp, yy * 2 + cc)

    def zpeer(d):
        return device(lax.rem(z + d, Z), pd, y, core)

    def pplace(d):
        q = lax.rem(plane + d, PLANE)
        return q // Y, lax.rem(q, Y)

    def ppeer(d):
        pp, yy = pplace(d)
        return device(z, pp, yy, core)

    sibling = device(z, pd, y, 1 - core)

    def cpeer(d):
        return (dp_i, lax.rem(col_i + d, 2 * Y))

    def remote(src, dst, send, recv, to):
        return pltpu.make_async_remote_copy(
            src_ref=src, dst_ref=dst, send_sem=send, recv_sem=recv, device_id=to, device_id_type=MESH)

    barrier = pltpu.get_barrier_semaphore()
    near = [zpeer(d) for d in range(1, Z)] + [ppeer(d) for d in range(1, PLANE)]
    near += [cpeer(d) for d in range(1, 2 * Y) if d != Y]
    for to in near + ([sibling] if Y == 1 else []):
        pl.semaphore_signal(barrier, inc=1, device_id=to, device_id_type=MESH)
    greeted = len(near)

    cin = pltpu.make_async_copy(tokens, x.at[pl.ds(0, rows)], csem.at[0])
    cup = pltpu.make_async_copy(upstream, up.at[pl.ds(0, rows)], csem.at[1])
    cin.start()
    cup.start()

    def padded(v):
        return v if RV == RB else jnp.concatenate([v, jnp.zeros((RB - RV, v.shape[1]), v.dtype)], axis=0)

    own = padded(packed[...].astype(F32))
    own = jnp.concatenate([own, jnp.zeros((RB, D - own.shape[1]), F32)], axis=1)
    frame[...] = pltpu.roll(own, 32 * col_i, 1)

    def turn(h):
        return lanes_of(lax.rem(h + col_i, 3), 128)

    for h in range(PAIRS):
        wpk[h, z, pd, :, lanes_of(pos, 128)] = frame[:, turn(h)].astype(BF16)
    own = padded(jnp.transpose(projection[...].astype(F32)))
    own = jnp.concatenate([own, jnp.zeros((RB, 128 - own.shape[1]), F32)], axis=1)
    ptr[z, pd, :, lanes_of(pos, 128)] = pltpu.roll(own, lax.rem(96 * col_i, 128), 1).astype(BF16)
    exr[z, pd, :, lanes_of(pos, D)] = padded(expansion[...])
    rtr[z, pd, :, lanes_of(pos, D)] = padded(jnp.transpose(reduction[...].astype(F32))).astype(BF16)
    vrow = jnp.concatenate([packed_bias[...].reshape(1, -1), jnp.zeros((1, D - packed_bias.shape[0]), F32)], axis=1)
    vrow = pltpu.roll(jnp.broadcast_to(vrow, (8, D)), 32 * col_i, 1)
    bias[pos] = jnp.concatenate([vrow[:4], jnp.broadcast_to(expansion_bias[...].reshape(1, -1), (4, D))], axis=0)

    chunks = [(wpk.at[h], 128) for h in range(PAIRS)] + [(ptr, 128), (exr, D), (rtr, D)]

    def zcopy(k, d):
        ref, width = chunks[k]
        slot = ref.at[z, pd, :, lanes_of(pos, width)]
        return remote(slot, slot, zs.at[k, d - 1], zr.at[k, d - 1], zpeer(d))

    def pcopy(k, d):
        ref, width = chunks[k]
        slot = ref.at[:, pd, :, lanes_of(pos, width)]
        return remote(slot, slot, ps.at[k, d - 1], pr.at[k, d - 1], ppeer(d))

    def kcopy(k):
        ref, width = chunks[k]
        slot = ref.at[:, :, :, lanes_of(core, Y * width)]
        return remote(slot, slot, ks.at[k], kr.at[k], sibling)

    def bcopy(d):
        return remote(bias.at[pos], bias.at[pos], bs.at[d - 1], br.at[d - 1], cpeer(d))

    def to_plane(k):
        for d in range(1, Z):
            zcopy(k, d).wait_recv()
        for d in range(1, PLANE):
            pcopy(k, d).start()

    def to_sibling(k):
        for d in range(1, PLANE):
            pcopy(k, d).wait_recv()
        kcopy(k).start()

    def settle(k):
        for d in range(1, Z):
            zcopy(k, d).wait_send()
        for d in range(1, PLANE):
            pcopy(k, d).wait_send()
        kcopy(k).wait_send()

    pl.semaphore_wait(barrier, greeted)
    for k in range(len(chunks)):
        for d in range(1, Z):
            zcopy(k, d).start()
        if k == 0:
            for d in range(1, 2 * Y):
                bcopy(d).start()

    x[rows:, :] = jnp.zeros((RP - rows, D), BF16)
    up[rows:, :] = jnp.zeros((RP - rows, D), BF16)
    for h in range(PAIRS):
        qkv[h, RP:, :] = jnp.zeros((qkv.shape[1] - RP, D), BF16)
    tail = attn.shape[0] - RP + 16
    attn[RP - 16:, :] = jnp.zeros((tail, D), BF16)
    ag[RP:, :] = jnp.zeros((ag.shape[0] - RP, D), BF16)
    rinv[RP - 16:, :] = jnp.zeros((tail, D), F32)
    pgr[:, RP - 16:, :] = jnp.zeros((PAIRS, tail, D), BF16)
    fs = first_scale[...].reshape(1, D)
    fh = first_shift[...].reshape(1, D)
    ss = second_scale[...].reshape(1, D)
    sh = second_shift[...].reshape(1, D)
    prb = projection_bias[...].reshape(1, D)
    rdb = reduction_bias[...].reshape(1, D)
    cin.wait()
    cup.wait()

    def ln1(i, _):
        s = rows_of(i, SMALL)
        v = x[s, :].astype(F32)
        avg = mean(v)
        inv = lax.rsqrt(mean(v * v) - avg * avg + EPS)
        normed = (v - avg) * inv
        n1[s, :] = normed
        inv1[s, :] = jnp.broadcast_to(inv, (SMALL, 128))
        rows1[s, :] = (normed * fs + fh).astype(BF16)
        hook(i, [(nsm // 2, lambda: to_plane(0))])
        return 0

    lax.fori_loop(0, nsm, ln1, 0)
    to_plane(1)
    to_sibling(0)
    to_plane(2)
    for d in range(1, 2 * Y):
        bcopy(d).wait_recv()

    lane = lax.broadcasted_iota(jnp.int32, (KEYS, 128), 1)
    even = lane < 64
    zero = jnp.zeros((KEYS, 128), BF16)
    one = jnp.ones((KEYS, 128), BF16)
    ones_e = jnp.where(even, one, zero)
    ones_o = jnp.where(even, zero, one)

    def place(c):
        return (c % 2) * Y + c // 2

    if RV != RB:
        wide = Z * PD * RB
        r_ = lax.broadcasted_iota(jnp.int32, (D, wide), 0)
        c_ = lax.broadcasted_iota(jnp.int32, (D, wide), 1)
        pick = jnp.where(c_ == (r_ // RV) * RB + lax.rem(r_, RV), 1.0, 0.0).astype(BF16)

    def compact(v):
        v = v.reshape(Z * PD * RB, v.shape[-1])
        return v if RV == RB else nn(pick, v).astype(BF16)

    def spread(v):
        v = v.astype(BF16)
        v = v if RV == RB else tn(pick, v).astype(BF16)
        return v.reshape(Z, PD, RB, v.shape[-1])

    def merged(tile, first, second, upto):
        if first == second:
            return tile(first)
        a, b = tile(first), tile(second)
        return jnp.where(lax.broadcasted_iota(jnp.int32, a.shape, 1) < upto, a, b)

    def assemble(h):
        kcopy(h).wait_recv()
        for j, (first, second, upto) in enumerate(TILES[h]):
            wp[h, :, j * 128:(j + 1) * 128] = merged(
                lambda c: compact(wpk[h, :, :, :, place(c) * 128:(place(c) + 1) * 128]), first, second, upto)

    def bias_of(h):
        def tile(c):
            t = (h + c) % 3
            return bias[place(c), 0:1, t * 128:(t + 1) * 128]
        return jnp.concatenate([merged(tile, *t) for t in TILES[h]], axis=1)

    def window(i):
        first = i * SEQ
        base = pl.multiple_of((first // 16) * 16, 16)
        return first - base, base

    ahead = (
        [(1, lambda: to_sibling(1)), (2, lambda: to_plane(3)), (3, lambda: to_plane(4)), (5, lambda: to_plane(5))],
        [(1, lambda: to_sibling(2)), (6, lambda: to_sibling(3))],
        [(2, lambda: to_sibling(4)), (6, lambda: to_sibling(5))],
    )
    for h in range(PAIRS):
        hl = pl.ds(h * 128, 128)
        assemble(h)
        pb = bias_of(h)

        def project(i, _):
            s = rows_of(i, BIG)
            qkv[h, s, :] = (nn(rows1[s, :], wp[h]) + pb).astype(BF16)
            return 0

        lax.fori_loop(0, nbig, project, 0)

        def attend(i, _):
            off, base = window(i)
            qs = pl.ds(base, WIN)
            kk = pl.ds(base, KEYS)
            q = qkv[h, qs, 0:128]
            k = qkv[h, kk, 128:256]
            v = qkv[h, kk, 256:384]
            col = lax.broadcasted_iota(jnp.int32, (WIN, KEYS), 1) - off
            ok = (col >= 0) & (col < SEQ)
            es = []
            for m in (even, ~even):
                s = nt(q, jnp.where(m, k, zero))
                s = jnp.where(ok, s, -1e30)
                top = jnp.max(s, axis=1, keepdims=True)
                es.append(jnp.exp((s - top) * 0.125).astype(BF16))
            est[h, i, 0] = es[0]
            est[h, i, 1] = es[1]
            mix = nn(es[0], jnp.concatenate([jnp.where(even, v, zero), ones_e], axis=1)) + nn(
                es[1], jnp.concatenate([jnp.where(even, zero, v), ones_o], axis=1))
            r = 1.0 / mix[:, 128:]
            o = mix[:, :128] * r
            rid = lax.broadcasted_iota(jnp.int32, (WIN, 128), 0) - off
            mine = (rid >= 0) & (rid < SEQ)
            attn[qs, hl] = jnp.where(mine, o, attn[qs, hl].astype(F32)).astype(BF16)
            rinv[qs, hl] = jnp.where(mine, r, rinv[qs, hl])
            hook(i, ahead[h])
            return 0

        lax.fori_loop(0, images, attend, 0)

    for k in (3, 4, 5):
        kcopy(k).wait_recv()
    lane_d = lax.broadcasted_iota(jnp.int32, (D, 128), 1)
    tiles = [compact(ptr[:, :, :, place(c) * 128:(place(c) + 1) * 128]) for c in range(4)]
    pt[:, 0:128] = jnp.where(lane_d < 96, tiles[0], tiles[1])
    pt[:, 128:256] = jnp.where(lane_d < 64, tiles[1], tiles[2])
    pt[:, 256:384] = jnp.where(lane_d < 32, tiles[2], tiles[3])
    if RV != RB:
        for c in range(0, FF, D):
            exc[:, c:c + D] = compact(exr[:, :, :, c:c + D])
            rtc[:, c:c + D] = compact(rtr[:, :, :, c:c + D])

    def ex_of(a, size):
        return exc[:, a:a + size] if RV != RB else exr[:, :, :, a:a + size].reshape(D, size)

    def rt_of(a, size):
        return rtc[:, a:a + size] if RV != RB else rtr[:, :, :, a:a + size].reshape(D, size)

    exb = jnp.concatenate([bias[p, 4:5, :] for p in range(4)], axis=1)
    acc2 = rg

    def ln2(i, _):
        s = rows_of(i, SMALL)
        v = x[s, :].astype(F32) + nt(attn[s, :], pt[...]) + prb
        avg = mean(v)
        inv = lax.rsqrt(mean(v * v) - avg * avg + EPS)
        normed = (v - avg) * inv
        acc1[s, :] = v + rdb
        n2[s, :] = normed
        inv2[s, :] = jnp.broadcast_to(inv, (SMALL, 128))
        rows2[s, :] = (normed * ss + sh).astype(BF16)
        acc2[s, :] = jnp.zeros((SMALL, D), F32)
        return 0

    lax.fori_loop(0, nsm, ln2, 0)

    SLOT = 2 * D + 128

    def put(lo, width, base, value):
        at = lo
        while at < lo + width:
            p, inner = at // D, at % D
            take = min(D - inner, lo + width - at)
            gm[:, :, :, p * SLOT + base + inner:p * SLOT + base + inner + take] = spread(value[:, at - lo:at - lo + take])
            at += take

    for c in range(FF // HC):
        lo = c * HC
        cs = pl.ds(lo, HC)

        def mlp(i, bsum):
            s = rows_of(i, BIG)
            pre = nn(rows2[s, :], ex_of(lo, HC)) + exb[:, lo:lo + HC]
            ug = nn(up[s, :], rt_of(lo, HC))
            cdf = 0.5 + 0.5 * lax.erf(pre * ROOT_HALF)
            act[s, :] = (pre * cdf).astype(BF16)
            g = ug * (cdf + pre * (jnp.exp(pre * pre * -0.5) * INV_ROOT_TAU))
            hg[s, :] = g.astype(BF16)
            acc1[s, :] += nt(act[s, :], rt_of(lo, HC))
            acc2[s, :] += nt(hg[s, :], ex_of(lo, HC))
            return bsum + jnp.sum(g, axis=0, keepdims=True)

        eb[0:1, cs] = lax.fori_loop(0, nbig, mlp, jnp.zeros((1, HC), F32))
        put(lo, HC, 0, tn(rows2[...], hg[...]))
        put(lo, HC, D, tn(up[...], act[...]))

    def ln2b(i, carry):
        s = rows_of(i, SMALL)
        u = up[s, :].astype(F32)
        x[s, :] = acc1[s, :].astype(BF16)
        g = acc2[s, :]
        normed = n2[s, :]
        inv = inv2[s, 0:1]
        scaled = g * ss
        d = u + inv * (scaled - mean(scaled) - normed * mean(scaled * normed))
        rg[s, :] = d
        rgb[s, :] = d.astype(BF16)
        ag[s, :] = nn(d.astype(BF16), pt[...]).astype(BF16)
        terms = (d, u, g * normed, g)
        return tuple(a + jnp.sum(t, axis=0, keepdims=True) for a, t in zip(carry, terms))

    zr1 = jnp.zeros((1, D), F32)
    sums = lax.fori_loop(0, nsm, ln2b, (zr1,) * 4)
    vec[...] = jnp.zeros(vec.shape, F32)
    for r, t in zip((0, 1, 4, 5), sums):
        vec[r:r + 1, :] = t
    gj = tn(rgb[...], attn[0:RP, :]).astype(BF16)
    t0, t1, t2 = gj[:, 0:128], gj[:, 128:256], gj[:, 256:384]
    for c, t in enumerate((t0, jnp.where(lane_d < 64, t1, t0), jnp.where(lane_d < 64, t2, t1), t2)):
        p = place(c) * SLOT
        gm[:, :, :, p + 2 * D:p + SLOT] = spread(t)
    cout = pltpu.make_async_copy(x.at[pl.ds(0, rows)], out_hbm, csem.at[0])
    cout.start()

    gsend = [gm] + [gh.at[h] for h in range(PAIRS)]
    r1s = [rm1] + [rh1.at[h] for h in range(PAIRS)]
    r2s = [rm2] + [rh2.at[h] for h in range(PAIRS)]
    r3s = [rm3] + [rh3.at[h] for h in range(PAIRS)]
    s1s = [sm1] + [sh1.at[h] for h in range(PAIRS)]
    s2s = [sm2] + [sh2.at[h] for h in range(PAIRS)]
    widths = [SLOT] + [128] * PAIRS

    def g1(k):
        half = Y * widths[k]
        return remote(gsend[k].at[:, :, :, lanes_of(1 - core, half)], r1s[k], gs.at[k, 0], gr_.at[k, 0], sibling)

    def g2(k, d):
        pp, yy = pplace(d)
        return remote(s1s[k].at[:, pp, :, lanes_of(yy, widths[k])], r2s[k].at[d - 1],
                      gs.at[k, d], gr_.at[k, d], ppeer(d))

    def g3(k, d):
        return remote(s2s[k].at[lax.rem(z + d, Z)], r3s[k].at[d - 1],
                      gs.at[k, PLANE - 1 + d], gr_.at[k, PLANE - 1 + d], zpeer(d))

    def sum1(k):
        half = Y * widths[k]
        g1(k).wait_recv()
        s1s[k][...] = (gsend[k][:, :, :, lanes_of(core, half)].astype(F32) + r1s[k][...].astype(F32)).astype(BF16)
        for d in range(1, PLANE):
            g2(k, d).start()

    def sum2(k):
        for d in range(1, PLANE):
            g2(k, d).wait_recv()
        total = s1s[k][:, pd, :, lanes_of(y, widths[k])].astype(F32)
        for d in range(1, PLANE):
            total += r2s[k][d - 1].astype(F32)
        s2s[k][...] = total.astype(BF16)
        for d in range(1, Z):
            g3(k, d).start()

    def sum3(k):
        for d in range(1, Z):
            g3(k, d).wait_recv()
        total = s2s[k][z].astype(F32)
        for d in range(1, Z):
            total += r3s[k][d - 1].astype(F32)
        return total

    def sent(k):
        g1(k).wait_send()
        for d in range(1, PLANE):
            g2(k, d).wait_send()
        for d in range(1, Z):
            g3(k, d).wait_send()

    g1(0).start()

    behind = (
        [(2, lambda: sum1(0))],
        [(0, lambda: sum1(1)), (3, lambda: sum2(0)), (6, lambda: sum2(1))],
        [(0, lambda: sum1(2)), (6, lambda: sum2(2))],
    )
    for h in range(PAIRS):
        hl = pl.ds(h * 128, 128)

        def attend_back(i, _):
            off, base = window(i)
            qs = pl.ds(base, WIN)
            kk = pl.ds(base, KEYS)
            q = qkv[h, qs, 0:128]
            k = qkv[h, kk, 128:256]
            v = qkv[h, kk, 256:384]
            rid = lax.broadcasted_iota(jnp.int32, (WIN, 128), 0) - off
            mine = (rid >= 0) & (rid < SEQ)
            do = jnp.where(mine, ag[qs, hl].astype(F32) * rinv[qs, hl], 0.0)
            dob = do.astype(BF16)
            xx = jnp.concatenate([dob, (do * attn[qs, hl].astype(F32)).astype(BF16)], axis=1)
            ev = even[:WIN]
            zw = zero[:WIN]
            e0 = est[h, i, 0]
            e1 = est[h, i, 1]
            d0 = (e0 * nt(xx, jnp.concatenate([jnp.where(even, v, zero), -ones_e], axis=1))).astype(BF16)
            d1 = (e1 * nt(xx, jnp.concatenate([jnp.where(even, zero, v), -ones_o], axis=1))).astype(BF16)
            dq = (nn(d0, jnp.where(even, k, zero)) + nn(d1, jnp.where(even, zero, k))) * 0.125
            dk = (tn(d0, jnp.where(ev, q, zw)) + tn(d1, jnp.where(ev, zw, q))) * 0.125
            dv = tn(e0, jnp.where(ev, dob, zw)) + tn(e1, jnp.where(ev, zw, dob))
            old = pgr[h, qs, :].astype(F32)
            pgr[h, qs, 0:128] = jnp.where(mine, dq, old[:, 0:128]).astype(BF16)
            pgr[h, qs, 128:256] = jnp.where(mine, dk[:WIN], old[:, 128:256]).astype(BF16)
            pgr[h, qs, 256:384] = jnp.where(mine, dv[:WIN], old[:, 256:384]).astype(BF16)
            hook(i, behind[h])
            return 0

        lax.fori_loop(0, images, attend_back, 0)
        gp = tn(rows1[...], pgr[h, 0:RP, :])
        for c, j in enumerate(SHARES[h]):
            gh[h, :, :, :, place(c) * 128:(place(c) + 1) * 128] = spread(gp[:, j * 128:(j + 1) * 128])
        g1(1 + h).start()

        def bias_sum(i, carry):
            s = rows_of(i, SMALL)
            return carry + jnp.sum(pgr[h, s, :].astype(F32), axis=0, keepdims=True)

        vec[6 + h:7 + h, :] = lax.fori_loop(0, nsm, bias_sum, zr1)

    def ln1b(i, carry):
        s = rows_of(i, SMALL)
        g = nt(pgr[0, s, :], wp[0]) + nt(pgr[1, s, :], wp[1]) + nt(pgr[2, s, :], wp[2])
        normed = n1[s, :]
        inv = inv1[s, 0:1]
        scaled = g * fs
        rg[s, :] = rg[s, :] + inv * (scaled - mean(scaled) - normed * mean(scaled * normed))
        terms = (g * normed, g)
        hook(i, [(3, lambda: sum1(3)), (nsm - 1, lambda: sum2(3))])
        return tuple(a + jnp.sum(t, axis=0, keepdims=True) for a, t in zip(carry, terms))

    sums = lax.fori_loop(0, nsm, ln1b, (zr1,) * 2)
    cg = pltpu.make_async_copy(rg.at[pl.ds(0, rows)], grad_hbm, csem.at[1])
    cg.start()

    for r, t in zip((2, 3), sums):
        vec[r:r + 1, :] = t
    for p in range(4):
        vec[9 + p:10 + p, :] = eb[0:1, p * D:(p + 1) * D]
    kv = len(gsend)

    def v1():
        return remote(vec, vr1, gs.at[kv, 0], gr_.at[kv, 0], sibling)

    def v2(d):
        return remote(vsum1, vr2.at[plane], gs.at[kv, d], gr_.at[kv, d], ppeer(d))

    def v3(d):
        return remote(vr3.at[z], vr3.at[z], gs.at[kv, PLANE - 1 + d], gr_.at[kv, PLANE - 1 + d], zpeer(d))

    v1().start()
    def finish_mlp():
        total = sum3(0)
        o_expansion[...] = total[:RV, 0:D]
        o_reduction[...] = jnp.transpose(total[:, D:2 * D])[:, :RV]
        t = pltpu.roll(total[:, 2 * D:], lax.rem(128 - lax.rem(96 * col_i, 128), 128), 1)
        o_projection[...] = jnp.transpose(t)[:96, :RV]

    finish_mlp()
    v1().wait_recv()
    vsum1[...] = vec[...] + vr1[...]
    for d in range(1, PLANE):
        v2(d).start()
    vr2[plane] = vsum1[...]
    for h in range(PAIRS - 1):
        frame[:, turn(h)] = sum3(1 + h)
    for d in range(1, PLANE):
        v2(d).wait_recv()
    total = vr2[0]
    for q in range(1, PLANE):
        total += vr2[q]
    vr3[z] = total
    for d in range(1, Z):
        v3(d).start()
    frame[:, turn(PAIRS - 1)] = sum3(PAIRS)
    back = lax.rem(D - 32 * col_i, D)
    wide_c = o_packed.shape[1]
    o_packed[...] = pltpu.roll(frame[...], back, 1)[:RV, :wide_c]
    for d in range(1, Z):
        v3(d).wait_recv()
    total = vr3[0]
    for q in range(1, Z):
        total += vr3[q]
    vec_all = total
    v1().wait_send()
    vec[...] = vec_all
    turned = pltpu.roll(vec_all[0:8, :], lax.rem(D - 96 * col_i, D), 1)
    for r, ref in enumerate((o_prb, o_rb, o_fs, o_fh, o_ss, o_sh)):
        ref[...] = turned[r:r + 1, :96].reshape(96)
    for h, j in enumerate((jnp.minimum(col_i, 2), (col_i + 1) // 2, jnp.maximum(col_i - 1, 0))):
        frame[0:1, turn(h)] = vec[6 + h:7 + h, lanes_of(j, 128)]
    o_pb[...] = pltpu.roll(frame[0:8, :], back, 1)[0:1, :wide_c].reshape(wide_c)
    o_eb[...] = vec[pl.ds(9 + pos, 1), :].reshape(D)

    for k in range(len(chunks)):
        settle(k)
    for d in range(1, 2 * Y):
        bcopy(d).wait_send()
    for k in range(len(gsend)):
        sent(k)
    for d in range(1, PLANE):
        v2(d).wait_send()
    for d in range(1, Z):
        v3(d).wait_send()
    cout.wait()
    cg.wait()


def finish_kernel(rows, *refs):
    n = 14
    ins, outs, (bx, bg, sem) = refs[:n], refs[n:2 * n], refs[2 * n:]
    a = pltpu.make_async_copy(ins[0], bx, sem.at[0])
    b = pltpu.make_async_copy(ins[1], bg, sem.at[1])
    a.start()
    b.start()
    for i in range(2, n):
        outs[i][...] = ins[i][...]
    a.wait()
    c = pltpu.make_async_copy(bx, outs[0], sem.at[0])
    c.start()
    b.wait()
    d = pltpu.make_async_copy(bg, outs[1], sem.at[1])
    d.start()
    c.wait()
    d.wait()


def body(dps, cols, tokens, packed, packed_bias, projection, projection_bias, expansion, expansion_bias, reduction,
         reduction_bias, first_scale, first_shift, second_scale, second_shift, upstream):
    args = (tokens, packed, packed_bias, projection, projection_bias, expansion, expansion_bias, reduction,
            reduction_bias, first_scale, first_shift, second_scale, second_shift, upstream)
    rows = tokens.shape[0]
    images = rows // SEQ
    Z = min(4, dps)
    PD = dps // Z
    Y = cols // 2
    RV = packed.shape[0]
    RB = -(-RV // 16) * 16
    PLANE = PD * Y
    RP = -(-rows // BIG) * BIG
    XP = RP + 80
    cfg = (Z, PD, Y, RB, RV, rows)
    V = pl.BlockSpec(memory_space=pltpu.VMEM)
    A = pl.BlockSpec(memory_space=pl.ANY)
    S = jax.ShapeDtypeStruct
    vm = pltpu.VMEM
    dma = pltpu.SemaphoreType.DMA
    SLOT = 2 * D + 128
    small = RV != RB
    outs = (
        S((rows, D), BF16), S((rows, D), F32),
        S(packed.shape, F32), S(projection.shape, F32), S(expansion.shape, F32), S(reduction.shape, F32),
        S(packed_bias.shape, F32), S((D // cols,), F32), S(expansion_bias.shape, F32),
    ) + (S((D // cols,), F32),) * 5
    scratch = [
        vm((RP, D), BF16), vm((RP, D), BF16),
        vm((RP, D), F32), vm((RP, D), BF16),
        vm((PAIRS, XP, D), BF16), vm((XP, D), BF16),
        vm((PAIRS, images, 2, WIN, KEYS), BF16), vm((XP, D), F32),
        vm((RP, D), F32), vm((RP, D), BF16),
        vm((RP, D), F32), vm((RP, D), F32),
        vm((RP, HC), BF16), vm((RP, HC), BF16),
        vm((RP, D), BF16), vm((XP, D), BF16),
        vm((PAIRS, XP, D), BF16), vm((RP, 128), F32), vm((RP, 128), F32),
        vm((PAIRS, Z, PD, RB, 4 * 128), BF16), vm((Z, PD, RB, 4 * 128), BF16),
        vm((Z, PD, RB, FF), BF16), vm((Z, PD, RB, FF), BF16),
        vm((PAIRS, D, D), BF16), vm((D, D), BF16),
        vm((D, FF) if small else (16, 128), BF16), vm((D, FF) if small else (16, 128), BF16),
        vm((4, 8, D), F32),
        vm((Z, PD, RB, 4 * SLOT), BF16), vm((PAIRS, Z, PD, RB, 4 * 128), BF16),
        vm((Z, PD, RB, Y * SLOT), BF16), vm((PLANE - 1, Z, RB, SLOT), BF16), vm((Z - 1, RB, SLOT), BF16),
        vm((PAIRS, Z, PD, RB, Y * 128), BF16), vm((PAIRS, PLANE - 1, Z, RB, 128), BF16), vm((PAIRS, Z - 1, RB, 128), BF16),
        vm((Z, PD, RB, Y * SLOT), BF16), vm((Z, RB, SLOT), BF16),
        vm((PAIRS, Z, PD, RB, Y * 128), BF16), vm((PAIRS, Z, RB, 128), BF16),
        vm((RB, D), F32), vm((16, D), F32), vm((16, D), F32),
        vm((16, D), F32), vm((PLANE, 16, D), F32), vm((Z, 16, D), F32), vm((8, FF), F32),
        dma((2,)), dma((6, Z - 1)), dma((6, Z - 1)), dma((6, PLANE - 1)), dma((6, PLANE - 1)), dma((6,)), dma((6,)),
        dma((2 * Y - 1,)), dma((2 * Y - 1,)), dma((5, PLANE + Z - 1)), dma((5, PLANE + Z - 1)),
    ]
    got = pl.pallas_call(
        functools.partial(layer_kernel, cfg),
        out_shape=outs,
        in_specs=[A] + [V] * 12 + [A],
        out_specs=(A, A) + (V,) * 12,
        scratch_shapes=scratch,
        compiler_params=pltpu.CompilerParams(vmem_limit_bytes=67043328, collective_id=0, has_side_effects=True),
    )(*args)
    return pl.pallas_call(
        functools.partial(finish_kernel, rows),
        out_shape=outs,
        in_specs=[A, A] + [V] * 12,
        out_specs=(A, A) + (V,) * 12,
        scratch_shapes=[vm((rows, D), BF16), vm((rows, D), F32), dma((2,))],
    )(*got)


def solution(mesh):
    placed = (
        P(("dp", "col"), None), P("dp", "col"), P("col"), P("col", "dp"), P(), P("dp", "col"), P("col"),
        P("col", "dp"), P(), P(), P(), P(), P(), P(("dp", "col"), None),
    )
    return jax.shard_map(
        functools.partial(body, mesh.shape["dp"], mesh.shape["col"]),
        mesh=mesh,
        in_specs=placed,
        out_specs=(
            P(("dp", "col"), None), P(("dp", "col"), None),
            P("dp", "col"), P("col", "dp"), P("dp", "col"), P("col", "dp"),
        ) + (P("col"),) * 8,
        check_vma=False,
    )
```

profile of v0, /device:TPU:0, one launch (start us, length us, event | category | flops | bytes accessed | tf_op | source)
XLA Modules:
  0.0 126.3 jit_solution(18089265075693426665)
XLA Ops:
  0.6 1.4 %copy.28.refs_3_ = bf16[96,48]{1,0:T(8,128)(2,1)} copy(bf16[96,48]{0,1:T(8,128)(2,1)} %param.17) | data formatting | bytes 18432 | tf_op args[3]
  2.1 1.5 %copy.29.refs_7_ = bf16[384,48]{1,0:T(8,128)(2,1)} copy(bf16[384,48]{0,1:T(8,128)(2,1)} %param.21) | data formatting | bytes 73728 | tf_op args[7]
  3.6 114.3 %shard_map.245 = (bf16[1576,384]{1,0:T(8,128)(2,1)}, f32[1576,384]{1,0:T(8,128)}, f32[48,288]{1,0:T(8,128)}, f32[96,48]{1,0:T(8,128)}, f32[48,384]{1,0:T(8,128)}...) custom-call(bf16[1576,384]{1,0:T(8,128)(2,1)} %refs_0_.1, ...), custom_call_target="tpu_custom_call" | custom-call | tf_op jit(solution)/shard_map/pallas_call | solution.py:674
  117.8 5.3 %shard_map.246 = (bf16[1576,384]{1,0:T(8,128)(2,1)}, f32[1576,384]{1,0:T(8,128)}, f32[48,288]{1,0:T(8,128)}, f32[96,48]{1,0:T(8,128)}, f32[48,384]{1,0:T(8,128)}...) custom-call(bf16[1576,384]{1,0:T(8,128)(2,1)} %get-tuple-element.28., ...), custom_call_target="tpu_custom_call" | custom-call | tf_op jit(solution)/shard_map/pallas_call | solution.py:682
  123.2 1.5 %copy.30 = f32[96,48]{0,1:T(8,128)} copy(f32[96,48]{1,0:T(8,128)} %get-tuple-element.45) | data formatting | bytes 36864 | tf_op jit(solution)/shard_map/pallas_call | solution.py:682
  124.7 1.7 %copy.31 = f32[384,48]{0,1:T(8,128)} copy(f32[384,48]{1,0:T(8,128)} %get-tuple-element.47) | data formatting | bytes 147456 | tf_op jit(solution)/shard_map/pallas_call | solution.py:682
where the time goes:
time: 127 us; the launch traced here: 126 us
  Pallas kernels  120 us (94%)
  local copies, waits for them, and re-layouts  6.08 us (5%)
    pallas_call x1, Pallas kernels, body(): pl.pallas_call(functools.partial(layer_kernel, cfg), out_shape=outs, in_s...  114 us
    pallas_call x1, Pallas kernels, body(): pl.pallas_call(functools.partial(finish_kernel, rows), out_shape=outs, in...  5.35 us
    pallas_call x2, local copies, waits for them, and re-layouts, body(): pl.pallas_call(functools.partial(finish_kernel, rows), out_shape=outs, in...  3.16 us
    unnamed x2, local copies, waits for them, and re-layouts  2.92 us

commit v1 on v0

v1 whole, which is shorter than its diff:
```python
import functools

import jax
import jax.numpy as jnp
from jax import lax
from jax.experimental import pallas as pl
from jax.experimental.pallas import tpu as pltpu
from jax.sharding import PartitionSpec as P

SEQ = 197
EPS = 1e-06
ROOT_HALF = 0.7071067811865476
INV_ROOT_TAU = 0.3989422804014327
F32, BF16 = jnp.float32, jnp.bfloat16
MESH = pl.DeviceIdType.MESH
D = 384
FF = 1536
PAIRS = 3
WIN = 224
KEYS = 256
BIG = 528
SMALL = 176
HC = 512


def nn(a, b):
    return lax.dot_general(a, b, (((1,), (0,)), ((), ())), preferred_element_type=F32)


def nt(a, b):
    return lax.dot_general(a, b, (((1,), (1,)), ((), ())), preferred_element_type=F32)


def tn(a, b):
    return lax.dot_general(a, b, (((0,), (0,)), ((), ())), preferred_element_type=F32)


def rows_of(i, size):
    return pl.ds(pl.multiple_of(i * size, 16), size)


def lanes_of(i, size):
    return pl.ds(pl.multiple_of(i * size, 128), size)


def mean(x):
    return jnp.sum(x, axis=1, keepdims=True) * (1.0 / x.shape[1])


def hook(i, steps):
    for at, step in steps:
        pl.when(i == at)(step)


def loop(lo, hi, function, init):
    with jax.named_scope(function.__name__):
        return lax.fori_loop(lo, hi, function, init)


def named(function):
    def inner(*a):
        with jax.named_scope(function.__name__ + "_".join(str(v) for v in a if isinstance(v, int))):
            return function(*a)
    return inner


TILES = (
    ((0, 0, 128), (1, 1, 128), (2, 3, 96)),
    ((0, 0, 128), (1, 2, 64), (3, 3, 128)),
    ((0, 1, 32), (2, 2, 128), (3, 3, 128)),
)
SHARES = ((0, 1, 2, 2), (0, 1, 1, 2), (0, 0, 1, 2))


def layer_kernel(cfg, *refs):
    Z, PD, Y, RB, RV, rows = cfg
    PLANE = PD * Y
    RP = -(-rows // BIG) * BIG
    images = rows // SEQ
    nsm, nbig = RP // SMALL, RP // BIG
    tokens, upstream, out_hbm, grad_hbm, small_hbm = refs[0], refs[13], refs[14], refs[15], refs[16]
    outside, refs = refs[1:13], refs[17:]
    (packed, packed_bias, projection, projection_bias, expansion, expansion_bias, reduction,
     reduction_bias, first_scale, first_shift, second_scale, second_shift, small,
     x, up, n1, rows1, qkv, attn, est, rinv, n2, rows2, acc1, rg, act, hg, rgb, ag, pgr, inv1, inv2,
     wpk, ptr, exr, rtr, wp, pt, exc, rtc, bias,
     gm, gh, rm1, rm2, rm3, rh1, rh2, rh3, sm1, sm2, sh1, sh2, frame, vec, vsum1, vr1, vr2, vr3, vall, gbuf,
     isem, csem, asend, zfirst, zr, pr, kr, bs, gsend, g1r, g2r, g3r, vs) = refs

    dp_i, col_i = lax.axis_index("dp"), lax.axis_index("col")
    z, pd = dp_i // PD, lax.rem(dp_i, PD)
    y, core = col_i // 2, lax.rem(col_i, 2)
    pos = core * Y + y
    plane = pd * Y + y

    def device(zz, pp, yy, cc):
        return (zz * PD + pp, yy * 2 + cc)

    def znear(s):
        rising = jnp.where(s < z, s, s + 1)
        down = Z - 1 - s
        falling = jnp.where(down > z, down, down - 1)
        return jnp.where(2 * z < Z, rising, falling)

    def zpeer(s):
        return device(znear(s - 1), pd, y, core)

    def pplace(d):
        q = lax.rem(plane + d, PLANE)
        return q // Y, lax.rem(q, Y)

    def ppeer(d):
        pp, yy = pplace(d)
        return device(z, pp, yy, core)

    sibling = device(z, pd, y, 1 - core)

    def cpeer(d):
        return (dp_i, lax.rem(col_i + d, 2 * Y))

    def remote(src, dst, send, recv, to):
        return pltpu.make_async_remote_copy(
            src_ref=src, dst_ref=dst, send_sem=send, recv_sem=recv, device_id=to, device_id_type=MESH)

    barrier = pltpu.get_barrier_semaphore()
    near = [zpeer(d) for d in range(1, Z)] + [ppeer(d) for d in range(1, PLANE)]
    near += [cpeer(d) for d in range(1, 2 * Y) if d != Y]
    for to in near + ([sibling] if Y == 1 else []):
        pl.semaphore_signal(barrier, inc=1, device_id=to, device_id_type=MESH)
    greeted = len(near)

    cin = pltpu.make_async_copy(tokens, x.at[pl.ds(0, rows)], csem.at[0])
    cup = pltpu.make_async_copy(upstream, up.at[pl.ds(0, rows)], csem.at[1])
    inside = (packed, packed_bias, projection, projection_bias, expansion, expansion_bias, reduction,
              reduction_bias, first_scale, first_shift, second_scale, second_shift)
    loads = [pltpu.make_async_copy(a, b, isem.at[n]) for n, (a, b) in enumerate(zip(outside, inside))]
    for n in (0, 2, 4, 6, 1, 5, 3, 7, 8, 9, 10, 11):
        loads[n].start()
    cin.start()
    cup.start()
    for load in loads:
        load.wait()

    def padded(v):
        return v if RV == RB else jnp.concatenate([v, jnp.zeros((RB - RV, v.shape[1]), v.dtype)], axis=0)

    own = padded(packed[...].astype(F32))
    own = jnp.concatenate([own, jnp.zeros((RB, D - own.shape[1]), F32)], axis=1)
    frame[...] = pltpu.roll(own, 32 * col_i, 1)

    def turn(h):
        return lanes_of(lax.rem(h + col_i, 3), 128)

    for h in range(PAIRS):
        wpk[h, z, pd, :, lanes_of(pos, 128)] = frame[:, turn(h)].astype(BF16)
    own = padded(projection[...].astype(F32))
    own = jnp.concatenate([own, jnp.zeros((RB, 128 - own.shape[1]), F32)], axis=1)
    ptr[z, pd, :, lanes_of(pos, 128)] = pltpu.roll(own, lax.rem(96 * col_i, 128), 1).astype(BF16)
    for j in range(FF // HC):
        exr[j, z, pd, :, lanes_of(pos, 128)] = padded(expansion[:, j * 128:(j + 1) * 128])
        rtr[j, z, pd, :, lanes_of(pos, 128)] = padded(reduction[:, j * 128:(j + 1) * 128])
    vrow = jnp.concatenate([packed_bias[...].reshape(1, -1), jnp.zeros((1, D - packed_bias.shape[0]), F32)], axis=1)
    vrow = pltpu.roll(jnp.broadcast_to(vrow, (8, D)), 32 * col_i, 1)
    bias[pos] = jnp.concatenate([vrow[:4], jnp.broadcast_to(expansion_bias[...].reshape(1, -1), (4, D))], axis=0)

    chunks = [wpk.at[h] for h in range(PAIRS)] + [ptr]
    for j in range(FF // HC):
        chunks += [exr.at[j], rtr.at[j]]
    mine_l = lanes_of(pos, 128)

    def span(slots):
        return inv1.at[0:slots * RB // 2]

    def vspan(count):
        return n1.at[0:count * 16]

    def arrived(sem, ref):
        remote(ref, ref, vs.at[0], sem, sibling).wait_recv()

    def left(sem, ref):
        remote(ref, ref, sem, vs.at[0], sibling).wait_send()

    def zcopy(k, d):
        slot = chunks[k].at[z, pd, :, mine_l]
        return remote(slot, slot, asend.at[k], zfirst.at[z] if k == 0 else zr.at[k], zpeer(d))

    def pcopy(k, d):
        slot = chunks[k].at[:, pd, :, mine_l]
        return remote(slot, slot, asend.at[k], pr.at[k], ppeer(d))

    def qcopy(d, q):
        slot = chunks[0].at[q, pd, :, mine_l]
        return remote(slot, slot, asend.at[0], pr.at[0], ppeer(d))

    def kcopy(k):
        slot = chunks[k].at[:, :, :, lanes_of(core, Y * 128)]
        return remote(slot, slot, asend.at[k], kr.at[k], sibling)

    def bcopy(d):
        return remote(bias.at[pos], bias.at[pos], bs.at[0], bs.at[1], cpeer(d))

    @named
    def to_plane(k):
        arrived(zr.at[k], span(Z - 1))
        for d in range(1, PLANE):
            pcopy(k, d).start()

    @named
    def to_sibling(k):
        arrived(pr.at[k], span((PLANE - 1) * Z))
        kcopy(k).start()

    ALL = Z - 1 + (PLANE - 1) * Z + PLANE * Z

    with jax.named_scope("barrier"):
        pl.semaphore_wait(barrier, greeted)
    for k in range(len(chunks)):
        for d in range(1, Z):
            zcopy(k, d).start()
        if k == 0:
            for d in range(1, PLANE):
                qcopy(d, z).start()
            for d in range(1, 2 * Y):
                bcopy(d).start()

    x[rows:, :] = jnp.zeros((RP - rows, D), BF16)
    up[rows:, :] = jnp.zeros((RP - rows, D), BF16)
    for h in range(PAIRS):
        qkv[h, RP:, :] = jnp.zeros((qkv.shape[1] - RP, D), BF16)
    tail = attn.shape[0] - RP + 16
    attn[RP - 16:, :] = jnp.zeros((tail, D), BF16)
    ag[RP:, :] = jnp.zeros((ag.shape[0] - RP, D), BF16)
    rinv[RP - 16:, :] = jnp.zeros((tail, D), F32)
    pgr[:, RP - 16:, :] = jnp.zeros((PAIRS, tail, D), BF16)
    fs = first_scale[...].reshape(1, D)
    fh = first_shift[...].reshape(1, D)
    ss = second_scale[...].reshape(1, D)
    sh = second_shift[...].reshape(1, D)
    prb = projection_bias[...].reshape(1, D)
    rdb = reduction_bias[...].reshape(1, D)
    cin.wait()
    cup.wait()

    def ln1(i, _):
        s = rows_of(i, SMALL)
        v = x[s, :].astype(F32)
        avg = mean(v)
        inv = lax.rsqrt(mean(v * v) - avg * avg + EPS)
        normed = (v - avg) * inv
        n1[s, :] = normed
        inv1[s, :] = jnp.broadcast_to(inv, (SMALL, 128))
        rows1[s, :] = (normed * fs + fh).astype(BF16)
        return 0

    @named
    def pass_on(d):
        q = znear(d - 1)
        arrived(zfirst.at[q], chunks[0].at[q, pd, :, mine_l])
        for e in range(1, PLANE):
            qcopy(e, q).start()

    loop(0, nsm, ln1, 0)
    for d in range(1, Z):
        pass_on(d)
    to_plane(1)
    with jax.named_scope("plane0"):
        arrived(pr.at[0], span((PLANE - 1) * Z))
    kcopy(0).start()
    to_plane(2)
    arrived(bs.at[1], n1.at[0:8 * (2 * Y - 1)])

    lane = lax.broadcasted_iota(jnp.int32, (KEYS, 128), 1)
    even = lane < 64
    zero = jnp.zeros((KEYS, 128), BF16)
    one = jnp.ones((KEYS, 128), BF16)
    ones_e = jnp.where(even, one, zero)
    ones_o = jnp.where(even, zero, one)

    def place(c):
        return (c % 2) * Y + c // 2

    if RV != RB:
        wide = Z * PD * RB
        r_ = lax.broadcasted_iota(jnp.int32, (D, wide), 0)
        c_ = lax.broadcasted_iota(jnp.int32, (D, wide), 1)
        pick = jnp.where(c_ == (r_ // RV) * RB + lax.rem(r_, RV), 1.0, 0.0).astype(BF16)

    def compact(v):
        v = v.reshape(Z * PD * RB, v.shape[-1])
        return v if RV == RB else nn(pick, v).astype(BF16)

    def spread(v):
        v = v.astype(BF16)
        v = v if RV == RB else tn(pick, v).astype(BF16)
        return v.reshape(Z, PD, RB, v.shape[-1])

    def merged(tile, first, second, upto):
        if first == second:
            return tile(first)
        a, b = tile(first), tile(second)
        return jnp.where(lax.broadcasted_iota(jnp.int32, a.shape, 1) < upto, a, b)

    @named
    def assemble(h):
        kcopy(h).wait_recv()
        for j, (first, second, upto) in enumerate(TILES[h]):
            wp[h, :, j * 128:(j + 1) * 128] = merged(
                lambda c: compact(wpk[h, :, :, :, place(c) * 128:(place(c) + 1) * 128]), first, second, upto)

    def bias_of(h):
        def tile(c):
            t = (h + c) % 3
            return bias[place(c), 0:1, t * 128:(t + 1) * 128]
        return jnp.concatenate([merged(tile, *t) for t in TILES[h]], axis=1)

    def window(i):
        first = i * SEQ
        base = pl.multiple_of((first // 16) * 16, 16)
        return first - base, base

    ahead = (
        [(1, lambda: to_sibling(1)), (2, lambda: to_plane(3)), (3, lambda: to_plane(4)), (4, lambda: to_plane(5)),
         (5, lambda: to_plane(6)), (6, lambda: to_plane(7)), (7, lambda: to_sibling(2))],
        [(1, lambda: to_plane(8)), (2, lambda: to_plane(9)), (4, lambda: to_sibling(3)), (7, lambda: to_sibling(4))],
        [(1, lambda: to_sibling(5)), (4, lambda: to_sibling(6)), (7, lambda: to_sibling(7))],
    )
    for h in range(PAIRS):
        hl = pl.ds(h * 128, 128)
        assemble(h)
        pb = bias_of(h)

        def project(i, _):
            s = rows_of(i, BIG)
            qkv[h, s, :] = (nn(rows1[s, :], wp[h]) + pb).astype(BF16)
            return 0

        loop(0, nbig, project, 0)

        def attend(i, _):
            off, base = window(i)
            qw = pl.ds(base, WIN)
            kk = pl.ds(base, KEYS)
            q = qkv[h, qw, 0:128]
            k = qkv[h, kk, 128:256]
            v = qkv[h, kk, 256:384]
            col = lax.broadcasted_iota(jnp.int32, (WIN, KEYS), 1) - off
            ok = (col >= 0) & (col < SEQ)
            es = []
            for m in (even, ~even):
                s = nt(q, jnp.where(m, k, zero))
                s = jnp.where(ok, s, -1e30)
                top = jnp.max(s, axis=1, keepdims=True)
                es.append(jnp.exp((s - top) * 0.125).astype(BF16))
            est[h, i, 0] = es[0]
            est[h, i, 1] = es[1]
            mix = nn(es[0], jnp.concatenate([jnp.where(even, v, zero), ones_e], axis=1)) + nn(
                es[1], jnp.concatenate([jnp.where(even, zero, v), ones_o], axis=1))
            r = 1.0 / mix[:, 128:]
            o = mix[:, :128] * r
            rid = lax.broadcasted_iota(jnp.int32, (WIN, 128), 0) - off
            mine = (rid >= 0) & (rid < SEQ)
            attn[qw, hl] = jnp.where(mine, o, attn[qw, hl].astype(F32)).astype(BF16)
            rinv[qw, hl] = jnp.where(mine, r, rinv[qw, hl])
            hook(i, ahead[h])
            return 0

        loop(0, images, attend, 0)

    kcopy(3).wait_recv()
    lane_d = lax.broadcasted_iota(jnp.int32, (D, 128), 1)
    tiles = [compact(ptr[:, :, :, place(c) * 128:(place(c) + 1) * 128]) for c in range(4)]
    pt[:, 0:128] = jnp.where(lane_d < 96, tiles[0], tiles[1])
    pt[:, 128:256] = jnp.where(lane_d < 64, tiles[1], tiles[2])
    pt[:, 256:384] = jnp.where(lane_d < 32, tiles[2], tiles[3])
    def exb_of(j):
        return jnp.concatenate([bias[p, 4:5, j * 128:(j + 1) * 128] for p in range(4)], axis=1)

    acc2 = rg

    def ln2(i, _):
        s = rows_of(i, SMALL)
        v = x[s, :].astype(F32) + nt(attn[s, :], pt[...]) + prb
        avg = mean(v)
        inv = lax.rsqrt(mean(v * v) - avg * avg + EPS)
        normed = (v - avg) * inv
        acc1[s, :] = v + rdb
        n2[s, :] = normed
        inv2[s, :] = jnp.broadcast_to(inv, (SMALL, 128))
        rows2[s, :] = (normed * ss + sh).astype(BF16)
        return 0

    loop(0, nsm, ln2, 0)

    def part(big, small, k):
        return big.at[k] if k < PAIRS else small.at[k - PAIRS]

    def width(k):
        return 256 if k < PAIRS else 128

    def g1(k):
        half = Y * width(k)
        return remote(part(gm, gh, k).at[:, :, :, lanes_of(1 - core, half)], part(rm1, rh1, k),
                      gsend.at[k], g1r.at[k], sibling)

    def g2(k, d):
        pp, yy = pplace(d)
        return remote(part(sm1, sh1, k).at[:, pp, :, lanes_of(yy, width(k))], part(rm2, rh2, k).at[d - 1],
                      gsend.at[k], g2r.at[k], ppeer(d))

    def g3(k, d):
        return remote(part(sm2, sh2, k).at[znear(d - 1)], part(rm3, rh3, k).at[z], gsend.at[k], g3r.at[k], zpeer(d))

    @named
    def sum1(k):
        g1(k).wait_recv()
        own = part(gm, gh, k)[:, :, :, lanes_of(core, Y * width(k))]
        part(sm1, sh1, k)[...] = (own.astype(F32) + part(rm1, rh1, k)[...].astype(F32)).astype(BF16)
        for d in range(1, PLANE):
            g2(k, d).start()

    @named
    def sum2(k):
        arrived(g2r.at[k], span((PLANE - 1) * Z * (width(k) // 128)))
        total = part(sm1, sh1, k)[:, pd, :, lanes_of(y, width(k))].astype(F32)
        for d in range(1, PLANE):
            total += part(rm2, rh2, k)[d - 1].astype(F32)
        part(sm2, sh2, k)[...] = total.astype(BF16)
        for d in range(1, Z):
            g3(k, d).start()

    @named
    def sum3(k):
        arrived(g3r.at[k], span((Z - 1) * (width(k) // 128)))
        total = part(sm2, sh2, k)[z].astype(F32)
        for d in range(1, Z):
            total += part(rm3, rh3, k)[znear(d - 1)].astype(F32)
        return total

    vec[...] = jnp.zeros(vec.shape, F32)
    spot = (
        [(1, lambda: to_sibling(8)), (2, lambda: to_sibling(9))],
        [(1, lambda: sum1(0))],
        [(1, lambda: sum1(1)), (2, lambda: sum2(0))],
    )
    for j in range(FF // HC):
        for k in (4 + 2 * j, 5 + 2 * j):
            kcopy(k).wait_recv()
        if RV != RB:
            exc[...] = compact(exr[j])
            rtc[...] = compact(rtr[j])

        def ex_of():
            return exc[...] if RV != RB else exr[j].reshape(D, HC)

        def rt_of():
            return rtc[...] if RV != RB else rtr[j].reshape(D, HC)

        exb = exb_of(j)

        def mlp(i, bsum):
            s = rows_of(i, BIG)
            pre = nn(rows2[s, :], ex_of()) + exb
            ug = nn(up[s, :], rt_of())
            cdf = 0.5 + 0.5 * lax.erf(pre * ROOT_HALF)
            act[s, :] = (pre * cdf).astype(BF16)
            g = ug * (cdf + pre * (jnp.exp(pre * pre * -0.5) * INV_ROOT_TAU))
            hg[s, :] = g.astype(BF16)
            acc1[s, :] += nt(act[s, :], rt_of())
            back = nt(hg[s, :], ex_of())
            acc2[s, :] = back if j == 0 else acc2[s, :] + back
            hook(i, spot[j])
            return bsum + jnp.sum(g, axis=0, keepdims=True)

        bsum = loop(0, nbig, mlp, jnp.zeros((1, HC), F32))
        for p in range(4):
            vec[9 + p:10 + p, j * 128:(j + 1) * 128] = bsum[:, p * 128:(p + 1) * 128]
        for base, g in ((0, tn(rows2[...], hg[...])), (128, tn(up[...], act[...]))):
            for p in range(4):
                gm[j, :, :, :, p * 256 + base:p * 256 + base + 128] = spread(g[:, p * 128:(p + 1) * 128])
        g1(j).start()

    def ln2b(i, carry):
        s = rows_of(i, SMALL)
        u = up[s, :].astype(F32)
        x[s, :] = acc1[s, :].astype(BF16)
        g = acc2[s, :]
        normed = n2[s, :]
        inv = inv2[s, 0:1]
        scaled = g * ss
        d = u + inv * (scaled - mean(scaled) - normed * mean(scaled * normed))
        rg[s, :] = d
        rgb[s, :] = d.astype(BF16)
        ag[s, :] = nn(d.astype(BF16), pt[...]).astype(BF16)
        terms = (d, u, g * normed, g)
        hook(i, [(nsm // 2, lambda: sum1(2)), (nsm - 1, lambda: sum2(1))])
        return tuple(a + jnp.sum(t, axis=0, keepdims=True) for a, t in zip(carry, terms))

    zr1 = jnp.zeros((1, D), F32)
    sums = loop(0, nsm, ln2b, (zr1,) * 4)
    for r, t in zip((0, 1, 4, 5), sums):
        vec[r:r + 1, :] = t
    gj = tn(rgb[...], attn[0:RP, :]).astype(BF16)
    t0, t1, t2 = gj[:, 0:128], gj[:, 128:256], gj[:, 256:384]
    for c, t in enumerate((t0, jnp.where(lane_d < 64, t1, t0), jnp.where(lane_d < 64, t2, t1), t2)):
        gh[0, :, :, :, place(c) * 128:(place(c) + 1) * 128] = spread(t)
    g1(3).start()
    cout = pltpu.make_async_copy(x.at[pl.ds(0, rows)], out_hbm, csem.at[0])
    cout.start()

    def finish_mlp(j):
        total = sum3(j)
        small[1, :, j * 128:(j + 1) * 128] = total[:, :128]
        small[2, :, j * 128:(j + 1) * 128] = total[:, 128:]

    def finish_projection():
        t = pltpu.roll(sum3(3), lax.rem(128 - lax.rem(96 * col_i, 128), 128), 1)
        small[3, :, 0:128] = t

    behind = (
        [(1, lambda: sum1(3)), (4, lambda: sum2(2)), (6, lambda: finish_mlp(0)), (7, lambda: sum2(3))],
        [(1, lambda: sum1(4)), (2, lambda: finish_mlp(1)), (4, lambda: finish_mlp(2)), (6, lambda: sum2(4))],
        [(1, lambda: sum1(5)), (2, lambda: finish_projection()), (6, lambda: sum2(5))],
    )
    for h in range(PAIRS):
        hl = pl.ds(h * 128, 128)

        def attend_back(i, _):
            off, base = window(i)
            qw = pl.ds(base, WIN)
            kk = pl.ds(base, KEYS)
            q = qkv[h, qw, 0:128]
            k = qkv[h, kk, 128:256]
            v = qkv[h, kk, 256:384]
            rid = lax.broadcasted_iota(jnp.int32, (WIN, 128), 0) - off
            mine = (rid >= 0) & (rid < SEQ)
            do = jnp.where(mine, ag[qw, hl].astype(F32) * rinv[qw, hl], 0.0)
            dob = do.astype(BF16)
            xx = jnp.concatenate([dob, (do * attn[qw, hl].astype(F32)).astype(BF16)], axis=1)
            ev = even[:WIN]
            zw = zero[:WIN]
            e0 = est[h, i, 0]
            e1 = est[h, i, 1]
            d0 = (e0 * nt(xx, jnp.concatenate([jnp.where(even, v, zero), -ones_e], axis=1))).astype(BF16)
            d1 = (e1 * nt(xx, jnp.concatenate([jnp.where(even, zero, v), -ones_o], axis=1))).astype(BF16)
            dq = (nn(d0, jnp.where(even, k, zero)) + nn(d1, jnp.where(even, zero, k))) * 0.125
            dk = (tn(d0, jnp.where(ev, q, zw)) + tn(d1, jnp.where(ev, zw, q))) * 0.125
            dv = tn(e0, jnp.where(ev, dob, zw)) + tn(e1, jnp.where(ev, zw, dob))
            old = pgr[h, qw, :].astype(F32)
            pgr[h, qw, 0:128] = jnp.where(mine, dq, old[:, 0:128]).astype(BF16)
            pgr[h, qw, 128:256] = jnp.where(mine, dk[:WIN], old[:, 128:256]).astype(BF16)
            pgr[h, qw, 256:384] = jnp.where(mine, dv[:WIN], old[:, 256:384]).astype(BF16)
            hook(i, behind[h])
            return 0

        loop(0, images, attend_back, 0)
        gp = tn(rows1[...], pgr[h, 0:RP, :])
        for c, j in enumerate(SHARES[h]):
            gh[1 + h, :, :, :, place(c) * 128:(place(c) + 1) * 128] = spread(gp[:, j * 128:(j + 1) * 128])
        g1(4 + h).start()

        def bias_sum(i, carry):
            s = rows_of(i, SMALL)
            return carry + jnp.sum(pgr[h, s, :].astype(F32), axis=0, keepdims=True)

        vec[6 + h:7 + h, :] = loop(0, nsm, bias_sum, zr1)

    def ln1b(i, carry):
        s = rows_of(i, SMALL)
        g = nt(pgr[0, s, :], wp[0]) + nt(pgr[1, s, :], wp[1]) + nt(pgr[2, s, :], wp[2])
        gbuf[s, :] = g
        terms = (g * n1[s, :], g)
        hook(i, [(nsm // 2, lambda: sum1(6))])
        return tuple(a + jnp.sum(t, axis=0, keepdims=True) for a, t in zip(carry, terms))

    sums = loop(0, nsm, ln1b, (zr1,) * 2)

    for r, t in zip((2, 3), sums):
        vec[r:r + 1, :] = t
    def v1():
        return remote(vec, vr1, vs.at[0], vs.at[1], sibling)

    def v2(d):
        return remote(vsum1, vr2.at[plane], vs.at[0], vs.at[2], ppeer(d))

    def v3(d):
        return remote(vr3.at[z], vr3.at[z], vs.at[0], vs.at[3], zpeer(d))

    def vector1():
        v1().wait_recv()
        vsum1[...] = vec[...] + vr1[...]
        for d in range(1, PLANE):
            v2(d).start()
        vr2[plane] = vsum1[...]

    def vector2():
        arrived(vs.at[2], vspan(PLANE - 1))
        total = vr2[0]
        for q in range(1, PLANE):
            total += vr2[q]
        vr3[z] = total
        for d in range(1, Z):
            v3(d).start()

    v1().start()

    def ln1c(i, _):
        s = rows_of(i, SMALL)
        normed = n1[s, :]
        inv = inv1[s, 0:1]
        scaled = gbuf[s, :] * fs
        rg[s, :] = rg[s, :] + inv * (scaled - mean(scaled) - normed * mean(scaled * normed))
        hook(i, [(nsm // 2 - 1, vector1), (nsm - 2, lambda: sum2(6)), (nsm - 1, vector2)])
        return 0

    loop(0, nsm, ln1c, 0)
    cg = pltpu.make_async_copy(rg.at[pl.ds(0, rows)], grad_hbm, csem.at[1])
    cg.start()
    for h in range(PAIRS):
        frame[:, turn(h)] = sum3(4 + h)
    back = lax.rem(D - 32 * col_i, D)
    small[0] = pltpu.roll(frame[...], back, 1)
    with jax.named_scope("vec3"):
        arrived(vs.at[3], vspan(Z - 1))
    total = vr3[0]
    for q in range(1, Z):
        total += vr3[q]
    vall[...] = total
    turned = pltpu.roll(total[0:8, :], lax.rem(D - 96 * col_i, D), 1)
    small[3, 0:8, 128:256] = turned[:, :128]
    for h, j in enumerate((jnp.minimum(col_i, 2), (col_i + 1) // 2, jnp.maximum(col_i - 1, 0))):
        frame[0:1, turn(h)] = vall[6 + h:7 + h, lanes_of(j, 128)]
    small[4, 0:8, :] = pltpu.roll(frame[0:8, :], back, 1)
    small[4, 8:9, :] = vall[pl.ds(9 + pos, 1), :]
    csmall = pltpu.make_async_copy(small, small_hbm, csem.at[2])
    csmall.start()

    with jax.named_scope("ends"):
        for k in range(len(chunks)):
            left(asend.at[k], span(ALL))
        left(bs.at[0], n1.at[0:8 * (2 * Y - 1)])
        for k in range(7):
            left(gsend.at[k], span(ALL * (width(k) // 128)))
        left(vs.at[0], vspan(PLANE + Z - 1))
        cout.wait()
        cg.wait()
        csmall.wait()


PIECES = 4


def finish_kernel(rows, *refs):
    rows_in, grad_in, small_in = refs[:3]
    outs, stage, (bx, bg, small, sem, osem, ssem) = refs[3:17], refs[17:29], refs[29:]
    step = -(-rows // (8 * PIECES)) * 8
    first = pltpu.make_async_copy(small_in, small, ssem.at[0])
    first.start()
    moves = []
    for c in range(PIECES):
        part = pl.ds(c * step, min(step, rows - c * step))
        for k, (src, buf, dst) in enumerate(((grad_in, bg, outs[1]), (rows_in, bx, outs[0]))):
            moves.append((
                pltpu.make_async_copy(src.at[part], buf.at[part], sem.at[0, k, c]),
                pltpu.make_async_copy(buf.at[part], dst.at[part], sem.at[1, k, c]),
            ))
    for take, _ in moves:
        take.start()
    first.wait()
    rv, wide = stage[0].shape
    stage[0][...] = small[0, :rv, :wide]
    stage[1][...] = small[3, :rv, :stage[1].shape[1]]
    stage[2][...] = small[1, :rv, :]
    stage[3][...] = small[2, :rv, :]
    stage[4][...] = small[4, 0:1, :wide].reshape(wide)
    stage[6][...] = small[4, 8:9, :].reshape(D)
    for r, k in enumerate((5, 7, 8, 9, 10, 11)):
        n = stage[k].shape[0]
        stage[k][...] = small[3, r:r + 1, 128:128 + n].reshape(n)
    gives = [pltpu.make_async_copy(stage[k], outs[2 + k], osem.at[k]) for k in range(12)]
    for give in gives:
        give.start()
    for take, give in moves:
        take.wait()
        give.start()
    for _, give in moves:
        give.wait()
    for give in gives:
        give.wait()


def body(dps, cols, tokens, packed, packed_bias, projection, projection_bias, expansion, expansion_bias, reduction,
         reduction_bias, first_scale, first_shift, second_scale, second_shift, upstream):
    args = (tokens, packed, packed_bias, projection.T, projection_bias, expansion, expansion_bias, reduction.T,
            reduction_bias, first_scale, first_shift, second_scale, second_shift, upstream)
    rows = tokens.shape[0]
    images = rows // SEQ
    Z = min(4, dps)
    PD = dps // Z
    Y = cols // 2
    RV = packed.shape[0]
    RB = -(-RV // 16) * 16
    PLANE = PD * Y
    RP = -(-rows // BIG) * BIG
    XP = RP + 80
    cfg = (Z, PD, Y, RB, RV, rows)
    V = pl.BlockSpec(memory_space=pltpu.VMEM)
    A = pl.BlockSpec(memory_space=pl.ANY)
    S = jax.ShapeDtypeStruct
    vm = pltpu.VMEM
    dma = pltpu.SemaphoreType.DMA
    NH = FF // HC
    NC = PAIRS + 1 + 2 * NH
    small = RV != RB
    outs = (
        S((rows, D), BF16), S((rows, D), F32),
        S(packed.shape, F32), S(projection.shape[::-1], F32), S(expansion.shape, F32), S(reduction.shape[::-1], F32),
        S(packed_bias.shape, F32), S((D // cols,), F32), S(expansion_bias.shape, F32),
    ) + (S((D // cols,), F32),) * 5
    narrow = (args[1], args[2], args[3], args[4], args[5], args[6], args[7]) + args[8:13]
    scratch = [vm(a.shape, a.dtype) for a in narrow] + [
        vm((5, RB, D), F32),
        vm((RP, D), BF16), vm((RP, D), BF16),
        vm((RP, D), F32), vm((RP, D), BF16),
        vm((PAIRS, XP, D), BF16), vm((XP, D), BF16),
        vm((PAIRS, images, 2, WIN, KEYS), BF16), vm((XP, D), F32),
        vm((RP, D), F32), vm((RP, D), BF16),
        vm((RP, D), F32), vm((RP, D), F32),
        vm((RP, HC), BF16), vm((RP, HC), BF16),
        vm((RP, D), BF16), vm((XP, D), BF16),
        vm((PAIRS, XP, D), BF16), vm((max(RP, (Z - 1 + (2 * PLANE - 1) * Z) * RB), 128), F32), vm((RP, 128), F32),
        vm((PAIRS, Z, PD, RB, 4 * 128), BF16), vm((Z, PD, RB, 4 * 128), BF16),
        vm((NH, Z, PD, RB, HC), BF16), vm((NH, Z, PD, RB, HC), BF16),
        vm((PAIRS, D, D), BF16), vm((D, D), BF16),
        vm((D, HC) if small else (16, 128), BF16), vm((D, HC) if small else (16, 128), BF16),
        vm((4, 8, D), F32),
        vm((NH, Z, PD, RB, 4 * 256), BF16), vm((4, Z, PD, RB, 4 * 128), BF16),
        vm((NH, Z, PD, RB, Y * 256), BF16), vm((NH, PLANE - 1, Z, RB, 256), BF16), vm((NH, Z, RB, 256), BF16),
        vm((4, Z, PD, RB, Y * 128), BF16), vm((4, PLANE - 1, Z, RB, 128), BF16), vm((4, Z, RB, 128), BF16),
        vm((NH, Z, PD, RB, Y * 256), BF16), vm((NH, Z, RB, 256), BF16),
        vm((4, Z, PD, RB, Y * 128), BF16), vm((4, Z, RB, 128), BF16),
        vm((RB, D), F32), vm((16, D), F32), vm((16, D), F32),
        vm((16, D), F32), vm((PLANE, 16, D), F32), vm((Z, 16, D), F32), vm((16, D), F32), vm((RP, D), F32),
        dma((12,)), dma((3,)), dma((NC,)), dma((Z,)), dma((NC,)), dma((NC,)), dma((NC,)),
        dma((2,)), dma((7,)), dma((7,)), dma((7,)), dma((7,)), dma((4,)),
    ]
    got = pl.pallas_call(
        functools.partial(layer_kernel, cfg),
        out_shape=(outs[0], outs[1], S((5, RB, D), F32)),
        in_specs=[A] * 14,
        out_specs=(A,) * 3,
        scratch_shapes=scratch,
        compiler_params=pltpu.CompilerParams(vmem_limit_bytes=67043328, collective_id=0, has_side_effects=True),
    )(*args)
    got = pl.pallas_call(
        functools.partial(finish_kernel, rows),
        out_shape=outs,
        in_specs=[A] * 3,
        out_specs=(A,) * 14,
        scratch_shapes=[vm(o.shape, o.dtype) for o in outs[2:]] + [
            vm((rows, D), BF16), vm((rows, D), F32), vm((5, RB, D), F32), dma((2, 2, PIECES)), dma((12,)), dma((1,))],
    )(*got)
    return got[:3] + (got[3].T, got[4], got[5].T) + tuple(got[6:])


def solution(mesh):
    placed = (
        P(("dp", "col"), None), P("dp", "col"), P("col"), P("col", "dp"), P(), P("dp", "col"), P("col"),
        P("col", "dp"), P(), P(), P(), P(), P(), P(("dp", "col"), None),
    )
    return jax.shard_map(
        functools.partial(body, mesh.shape["dp"], mesh.shape["col"]),
        mesh=mesh,
        in_specs=placed,
        out_specs=(
            P(("dp", "col"), None), P(("dp", "col"), None),
            P("dp", "col"), P("col", "dp"), P("dp", "col"), P("col", "dp"),
        ) + (P("col"),) * 8,
        check_vma=False,
    )
```

time: 127 us -> 105 us (0.83)
  Pallas kernels: 120 us -> 104 us
  local copies, waits for them, and re-layouts: 6.08 us -> 0 us
    pallas_call x1, Pallas kernels: 114 us -> 100 us  [body(): pl.pallas_call(functools.partial(layer_kernel, cfg), out_shape=(outs[0],...]
    pallas_call x2 -> x0, local copies, waits for them, and re-layouts: 3.16 us -> none  [body(): pl.pallas_call(functools.partial(finish_kernel, rows), out_shape=outs, in...]
    unnamed x2 -> x0, local copies, waits for them, and re-layouts: 2.92 us -> none
where the time goes in v1:
time: 105 us
  Pallas kernels  104 us (99%)
    pallas_call x1, Pallas kernels, body(): pl.pallas_call(functools.partial(layer_kernel, cfg), out_shape=(outs[0],...  100 us
    pallas_call x1, Pallas kernels, body(): pl.pallas_call(functools.partial(finish_kernel, rows), out_shape=outs, in...  4.2 us

profile of v1, /device:TPU:0, one launch (start us, length us, event | category | flops | bytes accessed | tf_op | source)
XLA Modules:
  0.0 105.1 jit_solution(6167886564368051550)
XLA Ops:
  0.7 100.1 %shard_map.245 = (bf16[1576,384]{1,0:T(8,128)(2,1)}, f32[1576,384]{1,0:T(8,128)}, f32[5,48,384]{2,1,0:T(8,128)}) custom-call(bf16[1576,384]{1,0:T(8,128)(2,1)} %refs_0_.1, bf16[48,288]{1,0:T(8,128)(2,1)} %refs_1_.1, f32[288]{0:T(512)} %refs_2_.1, bf16[48,96]{1,0:T(8,128)(2,1)} %bitcast.5, f32[384]{0:T(512)} %refs_4_.1, bf16[48,384]{1,0:T(8,128)(2,1)} %refs_5_.1, ...), custom_call_target="tpu_custom_call" | custom-call | tf_op jit(solution)/shard_map/pallas_call | solution.py:746
  100.7 4.2 %shard_map.246 = (bf16[1576,384]{1,0:T(8,128)(2,1)}, f32[1576,384]{1,0:T(8,128)}, f32[48,288]{1,0:T(8,128)}, f32[48,96]{1,0:T(8,128)}, f32[48,384]{1,0:T(8,128)}...) custom-call(bf16[1576,384]{1,0:T(8,128)(2,1)} %get-tuple-element.31., ...), custom_call_target="tpu_custom_call" | custom-call | tf_op jit(solution)/shard_map/pallas_call | solution.py:754

commit v2 on v1

--- a/solution.py
+++ b/solution.py
@@ -21,6 +21,7 @@
 BIG = 528
 SMALL = 176
 HC = 512
+LIMIT = 60 * 1024 * 1024
 
 
 def nn(a, b):
@@ -36,6 +37,8 @@
 
 
 def rows_of(i, size):
+    if isinstance(i, int):
+        return pl.ds(i * size, size)
     return pl.ds(pl.multiple_of(i * size, 16), size)
 
 
@@ -49,7 +52,18 @@
 
 def hook(i, steps):
     for at, step in steps:
-        pl.when(i == at)(step)
+        if isinstance(i, int):
+            if i == at:
+                step()
+        else:
+            pl.when(i == at)(lambda step=step: (step(), None)[1])
+
+
+def unrolled(lo, hi, function, init):
+    with jax.named_scope(function.__name__):
+        for i in range(lo, hi):
+            init = function(i, init)
+    return init
 
 
 def loop(lo, hi, function, init):
@@ -78,13 +92,13 @@
     RP = -(-rows // BIG) * BIG
     images = rows // SEQ
     nsm, nbig = RP // SMALL, RP // BIG
-    tokens, upstream, out_hbm, grad_hbm, small_hbm = refs[0], refs[13], refs[14], refs[15], refs[16]
-    outside, refs = refs[1:13], refs[17:]
+    tokens, upstream, outside = refs[0], refs[13], refs[1:13]
+    o_out, o_grad, small, refs = refs[14], refs[15], refs[16], refs[17:]
     (packed, packed_bias, projection, projection_bias, expansion, expansion_bias, reduction,
-     reduction_bias, first_scale, first_shift, second_scale, second_shift, small,
-     x, up, n1, rows1, qkv, attn, est, rinv, n2, rows2, acc1, rg, act, hg, rgb, ag, pgr, inv1, inv2,
+     reduction_bias, first_scale, first_shift, second_scale, second_shift,
+     x, up, n1, rows1, qkv, attn, est, rinv, n2, rows2, acc1, rg, act, hg, pgr, inv1, inv2,
      wpk, ptr, exr, rtr, wp, pt, exc, rtc, bias,
-     gm, gh, rm1, rm2, rm3, rh1, rh2, rh3, sm1, sm2, sh1, sh2, frame, vec, vsum1, vr1, vr2, vr3, vall, gbuf,
+     gm, gh, rm1, rm2, rm3, rh1, rh2, rh3, sm1, sm2, sh1, sh2, frame, vec, vsum1, vr1, vr2, vr3, vall,
      isem, csem, asend, zfirst, zr, pr, kr, bs, gsend, g1r, g2r, g3r, vs) = refs
 
     dp_i, col_i = lax.axis_index("dp"), lax.axis_index("col")
@@ -214,14 +228,15 @@
 
     with jax.named_scope("barrier"):
         pl.semaphore_wait(barrier, greeted)
-    for k in range(len(chunks)):
+    def to_z(k):
         for d in range(1, Z):
             zcopy(k, d).start()
-        if k == 0:
-            for d in range(1, PLANE):
-                qcopy(d, z).start()
-            for d in range(1, 2 * Y):
-                bcopy(d).start()
+
+    to_z(0)
+    for d in range(1, PLANE):
+        qcopy(d, z).start()
+    for d in range(1, 2 * Y):
+        bcopy(d).start()
 
     x[rows:, :] = jnp.zeros((RP - rows, D), BF16)
     up[rows:, :] = jnp.zeros((RP - rows, D), BF16)
@@ -229,7 +244,7 @@
         qkv[h, RP:, :] = jnp.zeros((qkv.shape[1] - RP, D), BF16)
     tail = attn.shape[0] - RP + 16
     attn[RP - 16:, :] = jnp.zeros((tail, D), BF16)
-    ag[RP:, :] = jnp.zeros((ag.shape[0] - RP, D), BF16)
+    act[RP:, :] = jnp.zeros((act.shape[0] - RP, HC), BF16)
     rinv[RP - 16:, :] = jnp.zeros((tail, D), F32)
     pgr[:, RP - 16:, :] = jnp.zeros((PAIRS, tail, D), BF16)
     fs = first_scale[...].reshape(1, D)
@@ -260,13 +275,15 @@
             qcopy(e, q).start()
 
     loop(0, nsm, ln1, 0)
+    to_z(1)
     for d in range(1, Z):
         pass_on(d)
+    for k in range(2, len(chunks)):
+        to_z(k)
     to_plane(1)
     with jax.named_scope("plane0"):
         arrived(pr.at[0], span((PLANE - 1) * Z))
     kcopy(0).start()
-    to_plane(2)
     arrived(bs.at[1], n1.at[0:8 * (2 * Y - 1)])
 
     lane = lax.broadcasted_iota(jnp.int32, (KEYS, 128), 1)
@@ -313,17 +330,22 @@
             return bias[place(c), 0:1, t * 128:(t + 1) * 128]
         return jnp.concatenate([merged(tile, *t) for t in TILES[h]], axis=1)
 
+    def keep(ref, i, value):
+        last = min(rows, (i + 1) * SMALL)
+        ref[i * SMALL:last, :] = value[:last - i * SMALL]
+
     def window(i):
         first = i * SEQ
-        base = pl.multiple_of((first // 16) * 16, 16)
-        return first - base, base
-
-    ahead = (
-        [(1, lambda: to_sibling(1)), (2, lambda: to_plane(3)), (3, lambda: to_plane(4)), (4, lambda: to_plane(5)),
-         (5, lambda: to_plane(6)), (6, lambda: to_plane(7)), (7, lambda: to_sibling(2))],
-        [(1, lambda: to_plane(8)), (2, lambda: to_plane(9)), (4, lambda: to_sibling(3)), (7, lambda: to_sibling(4))],
-        [(1, lambda: to_sibling(5)), (4, lambda: to_sibling(6)), (7, lambda: to_sibling(7))],
-    )
+        base = (first // 16) * 16
+        return first - base, base if isinstance(i, int) else pl.multiple_of(base, 16)
+
+    before = ((to_sibling, 1), (to_plane, 2)), ((to_sibling, 2),), ((to_sibling, 3),)
+    after = (tuple((to_plane, k) for k in (3, 4, 5, 6)), tuple((to_plane, k) for k in (7, 8, 9)), ((to_sibling, 4), (to_sibling, 5)))
+
+    def do(steps):
+        for step, k in steps:
+            step(k)
+
     for h in range(PAIRS):
         hl = pl.ds(h * 128, 128)
         assemble(h)
@@ -361,10 +383,11 @@
             mine = (rid >= 0) & (rid < SEQ)
             attn[qw, hl] = jnp.where(mine, o, attn[qw, hl].astype(F32)).astype(BF16)
             rinv[qw, hl] = jnp.where(mine, r, rinv[qw, hl])
-            hook(i, ahead[h])
             return 0
 
-        loop(0, images, attend, 0)
+        do(before[h])
+        unrolled(0, images, attend, 0)
+        do(after[h])
 
     kcopy(3).wait_recv()
     lane_d = lax.broadcasted_iota(jnp.int32, (D, 128), 1)
@@ -389,7 +412,7 @@
         rows2[s, :] = (normed * ss + sh).astype(BF16)
         return 0
 
-    loop(0, nsm, ln2, 0)
+    unrolled(0, nsm, ln2, 0)
 
     def part(big, small, k):
         return big.at[k] if k < PAIRS else small.at[k - PAIRS]
@@ -438,9 +461,9 @@
 
     vec[...] = jnp.zeros(vec.shape, F32)
     spot = (
-        [(1, lambda: to_sibling(8)), (2, lambda: to_sibling(9))],
-        [(1, lambda: sum1(0))],
-        [(1, lambda: sum1(1)), (2, lambda: sum2(0))],
+        ((to_sibling, 6), (to_sibling, 7)),
+        ((to_sibling, 8), (to_sibling, 9), (sum1, 0)),
+        ((sum1, 1),),
     )
     for j in range(FF // HC):
         for k in (4 + 2 * j, 5 + 2 * j):
@@ -468,13 +491,13 @@
             acc1[s, :] += nt(act[s, :], rt_of())
             back = nt(hg[s, :], ex_of())
             acc2[s, :] = back if j == 0 else acc2[s, :] + back
-            hook(i, spot[j])
             return bsum + jnp.sum(g, axis=0, keepdims=True)
 
         bsum = loop(0, nbig, mlp, jnp.zeros((1, HC), F32))
+        do(spot[j])
         for p in range(4):
             vec[9 + p:10 + p, j * 128:(j + 1) * 128] = bsum[:, p * 128:(p + 1) * 128]
-        for base, g in ((0, tn(rows2[...], hg[...])), (128, tn(up[...], act[...]))):
+        for base, g in ((0, tn(rows2[...], hg[...])), (128, tn(up[...], act[0:RP, :]))):
             for p in range(4):
                 gm[j, :, :, :, p * 256 + base:p * 256 + base + 128] = spread(g[:, p * 128:(p + 1) * 128])
         g1(j).start()
@@ -482,44 +505,43 @@
     def ln2b(i, carry):
         s = rows_of(i, SMALL)
         u = up[s, :].astype(F32)
-        x[s, :] = acc1[s, :].astype(BF16)
+        keep(o_out, i, acc1[s, :].astype(BF16))
         g = acc2[s, :]
         normed = n2[s, :]
         inv = inv2[s, 0:1]
         scaled = g * ss
         d = u + inv * (scaled - mean(scaled) - normed * mean(scaled * normed))
         rg[s, :] = d
-        rgb[s, :] = d.astype(BF16)
-        ag[s, :] = nn(d.astype(BF16), pt[...]).astype(BF16)
+        hg[s, 0:D] = d.astype(BF16)
+        act[s, 0:D] = nn(d.astype(BF16), pt[...]).astype(BF16)
         terms = (d, u, g * normed, g)
-        hook(i, [(nsm // 2, lambda: sum1(2)), (nsm - 1, lambda: sum2(1))])
         return tuple(a + jnp.sum(t, axis=0, keepdims=True) for a, t in zip(carry, terms))
 
     zr1 = jnp.zeros((1, D), F32)
-    sums = loop(0, nsm, ln2b, (zr1,) * 4)
+    sums = unrolled(0, nsm, ln2b, (zr1,) * 4)
     for r, t in zip((0, 1, 4, 5), sums):
         vec[r:r + 1, :] = t
-    gj = tn(rgb[...], attn[0:RP, :]).astype(BF16)
+    sum1(2)
+    sum2(0)
+    gj = tn(hg[:, 0:D], attn[0:RP, :]).astype(BF16)
     t0, t1, t2 = gj[:, 0:128], gj[:, 128:256], gj[:, 256:384]
     for c, t in enumerate((t0, jnp.where(lane_d < 64, t1, t0), jnp.where(lane_d < 64, t2, t1), t2)):
         gh[0, :, :, :, place(c) * 128:(place(c) + 1) * 128] = spread(t)
     g1(3).start()
-    cout = pltpu.make_async_copy(x.at[pl.ds(0, rows)], out_hbm, csem.at[0])
-    cout.start()
 
     def finish_mlp(j):
         total = sum3(j)
         small[1, :, j * 128:(j + 1) * 128] = total[:, :128]
         small[2, :, j * 128:(j + 1) * 128] = total[:, 128:]
 
-    def finish_projection():
+    def finish_projection(_):
         t = pltpu.roll(sum3(3), lax.rem(128 - lax.rem(96 * col_i, 128), 128), 1)
         small[3, :, 0:128] = t
 
     behind = (
-        [(1, lambda: sum1(3)), (4, lambda: sum2(2)), (6, lambda: finish_mlp(0)), (7, lambda: sum2(3))],
-        [(1, lambda: sum1(4)), (2, lambda: finish_mlp(1)), (4, lambda: finish_mlp(2)), (6, lambda: sum2(4))],
-        [(1, lambda: sum1(5)), (2, lambda: finish_projection()), (6, lambda: sum2(5))],
+        ((sum1, 3), (sum2, 1)),
+        ((sum1, 4), (sum2, 2), (sum2, 3), (finish_mlp, 0)),
+        ((sum1, 5), (sum2, 4), (finish_mlp, 1)),
     )
     for h in range(PAIRS):
         hl = pl.ds(h * 128, 128)
@@ -533,7 +555,7 @@
             v = qkv[h, kk, 256:384]
             rid = lax.broadcasted_iota(jnp.int32, (WIN, 128), 0) - off
             mine = (rid >= 0) & (rid < SEQ)
-            do = jnp.where(mine, ag[qw, hl].astype(F32) * rinv[qw, hl], 0.0)
+            do = jnp.where(mine, act[qw, hl].astype(F32) * rinv[qw, hl], 0.0)
             dob = do.astype(BF16)
             xx = jnp.concatenate([dob, (do * attn[qw, hl].astype(F32)).astype(BF16)], axis=1)
             ev = even[:WIN]
@@ -549,10 +571,10 @@
             pgr[h, qw, 0:128] = jnp.where(mine, dq, old[:, 0:128]).astype(BF16)
             pgr[h, qw, 128:256] = jnp.where(mine, dk[:WIN], old[:, 128:256]).astype(BF16)
             pgr[h, qw, 256:384] = jnp.where(mine, dv[:WIN], old[:, 256:384]).astype(BF16)
-            hook(i, behind[h])
             return 0
 
-        loop(0, images, attend_back, 0)
+        unrolled(0, images, attend_back, 0)
+        do(behind[h])
         gp = tn(rows1[...], pgr[h, 0:RP, :])
         for c, j in enumerate(SHARES[h]):
             gh[1 + h, :, :, :, place(c) * 128:(place(c) + 1) * 128] = spread(gp[:, j * 128:(j + 1) * 128])
@@ -562,7 +584,9 @@
             s = rows_of(i, SMALL)
             return carry + jnp.sum(pgr[h, s, :].astype(F32), axis=0, keepdims=True)
 
-        vec[6 + h:7 + h, :] = loop(0, nsm, bias_sum, zr1)
+        vec[6 + h:7 + h, :] = unrolled(0, nsm, bias_sum, zr1)
+
+    gbuf = acc1
 
     def ln1b(i, carry):
         s = rows_of(i, SMALL)
@@ -572,7 +596,7 @@
         hook(i, [(nsm // 2, lambda: sum1(6))])
         return tuple(a + jnp.sum(t, axis=0, keepdims=True) for a, t in zip(carry, terms))
 
-    sums = loop(0, nsm, ln1b, (zr1,) * 2)
+    sums = unrolled(0, nsm, ln1b, (zr1,) * 2)
 
     for r, t in zip((2, 3), sums):
         vec[r:r + 1, :] = t
@@ -608,15 +632,18 @@
         normed = n1[s, :]
         inv = inv1[s, 0:1]
         scaled = gbuf[s, :] * fs
-        rg[s, :] = rg[s, :] + inv * (scaled - mean(scaled) - normed * mean(scaled * normed))
-        hook(i, [(nsm // 2 - 1, vector1), (nsm - 2, lambda: sum2(6)), (nsm - 1, vector2)])
+        keep(o_grad, i, rg[s, :] + inv * (scaled - mean(scaled) - normed * mean(scaled * normed)))
+        hook(i, [(nsm // 2, vector1)])
         return 0
 
-    loop(0, nsm, ln1c, 0)
-    cg = pltpu.make_async_copy(rg.at[pl.ds(0, rows)], grad_hbm, csem.at[1])
-    cg.start()
-    for h in range(PAIRS):
+    unrolled(0, nsm, ln1c, 0)
+    do(((sum2, 5), (sum2, 6)))
+    with jax.named_scope("vector2"):
+        vector2()
+    do(((finish_mlp, 2), (finish_projection, 3)))
+    for h in range(PAIRS - 1):
         frame[:, turn(h)] = sum3(4 + h)
+    frame[:, turn(PAIRS - 1)] = sum3(3 + PAIRS)
     back = lax.rem(D - 32 * col_i, D)
     small[0] = pltpu.roll(frame[...], back, 1)
     with jax.named_scope("vec3"):
@@ -631,8 +658,6 @@
         frame[0:1, turn(h)] = vall[6 + h:7 + h, lanes_of(j, 128)]
     small[4, 0:8, :] = pltpu.roll(frame[0:8, :], back, 1)
     small[4, 8:9, :] = vall[pl.ds(9 + pos, 1), :]
-    csmall = pltpu.make_async_copy(small, small_hbm, csem.at[2])
-    csmall.start()
 
     with jax.named_scope("ends"):
         for k in range(len(chunks)):
@@ -641,31 +666,14 @@
         for k in range(7):
             left(gsend.at[k], span(ALL * (width(k) // 128)))
         left(vs.at[0], vspan(PLANE + Z - 1))
-        cout.wait()
-        cg.wait()
-        csmall.wait()
-
-
-PIECES = 4
-
-
-def finish_kernel(rows, *refs):
-    rows_in, grad_in, small_in = refs[:3]
-    outs, stage, (bx, bg, small, sem, osem, ssem) = refs[3:17], refs[17:29], refs[29:]
-    step = -(-rows // (8 * PIECES)) * 8
-    first = pltpu.make_async_copy(small_in, small, ssem.at[0])
-    first.start()
-    moves = []
-    for c in range(PIECES):
-        part = pl.ds(c * step, min(step, rows - c * step))
-        for k, (src, buf, dst) in enumerate(((grad_in, bg, outs[1]), (rows_in, bx, outs[0]))):
-            moves.append((
-                pltpu.make_async_copy(src.at[part], buf.at[part], sem.at[0, k, c]),
-                pltpu.make_async_copy(buf.at[part], dst.at[part], sem.at[1, k, c]),
-            ))
-    for take, _ in moves:
-        take.start()
-    first.wait()
+
+
+def finish_kernel(*refs):
+    out, grad, small = refs[:3]
+    outs, stage, sem = refs[3:17], refs[17:29], refs[29]
+    moves = [pltpu.make_async_copy(a, b, sem.at[k]) for k, (a, b) in enumerate(zip((grad, out) + stage, (outs[1], outs[0]) + outs[2:]))]
+    moves[0].start()
+    moves[1].start()
     rv, wide = stage[0].shape
     stage[0][...] = small[0, :rv, :wide]
     stage[1][...] = small[3, :rv, :stage[1].shape[1]]
@@ -676,16 +684,10 @@
     for r, k in enumerate((5, 7, 8, 9, 10, 11)):
         n = stage[k].shape[0]
         stage[k][...] = small[3, r:r + 1, 128:128 + n].reshape(n)
-    gives = [pltpu.make_async_copy(stage[k], outs[2 + k], osem.at[k]) for k in range(12)]
-    for give in gives:
-        give.start()
-    for take, give in moves:
-        take.wait()
-        give.start()
-    for _, give in moves:
-        give.wait()
-    for give in gives:
-        give.wait()
+    for move in moves[2:]:
+        move.start()
+    for move in moves:
+        move.wait()
 
 
 def body(dps, cols, tokens, packed, packed_bias, projection, projection_bias, expansion, expansion_bias, reduction,
@@ -718,15 +720,13 @@
     ) + (S((D // cols,), F32),) * 5
     narrow = (args[1], args[2], args[3], args[4], args[5], args[6], args[7]) + args[8:13]
     scratch = [vm(a.shape, a.dtype) for a in narrow] + [
-        vm((5, RB, D), F32),
         vm((RP, D), BF16), vm((RP, D), BF16),
         vm((RP, D), F32), vm((RP, D), BF16),
         vm((PAIRS, XP, D), BF16), vm((XP, D), BF16),
         vm((PAIRS, images, 2, WIN, KEYS), BF16), vm((XP, D), F32),
         vm((RP, D), F32), vm((RP, D), BF16),
         vm((RP, D), F32), vm((RP, D), F32),
-        vm((RP, HC), BF16), vm((RP, HC), BF16),
-        vm((RP, D), BF16), vm((XP, D), BF16),
+        vm((XP, HC), BF16), vm((RP, HC), BF16),
         vm((PAIRS, XP, D), BF16), vm((max(RP, (Z - 1 + (2 * PLANE - 1) * Z) * RB), 128), F32), vm((RP, 128), F32),
         vm((PAIRS, Z, PD, RB, 4 * 128), BF16), vm((Z, PD, RB, 4 * 128), BF16),
         vm((NH, Z, PD, RB, HC), BF16), vm((NH, Z, PD, RB, HC), BF16),
@@ -739,26 +739,26 @@
         vm((NH, Z, PD, RB, Y * 256), BF16), vm((NH, Z, RB, 256), BF16),
         vm((4, Z, PD, RB, Y * 128), BF16), vm((4, Z, RB, 128), BF16),
         vm((RB, D), F32), vm((16, D), F32), vm((16, D), F32),
-        vm((16, D), F32), vm((PLANE, 16, D), F32), vm((Z, 16, D), F32), vm((16, D), F32), vm((RP, D), F32),
-        dma((12,)), dma((3,)), dma((NC,)), dma((Z,)), dma((NC,)), dma((NC,)), dma((NC,)),
+        vm((16, D), F32), vm((PLANE, 16, D), F32), vm((Z, 16, D), F32), vm((16, D), F32),
+        dma((12,)), dma((2,)), dma((NC,)), dma((Z,)), dma((NC,)), dma((NC,)), dma((NC,)),
         dma((2,)), dma((7,)), dma((7,)), dma((7,)), dma((7,)), dma((4,)),
     ]
     got = pl.pallas_call(
         functools.partial(layer_kernel, cfg),
-        out_shape=(outs[0], outs[1], S((5, RB, D), F32)),
+        out_shape=(vm((rows, D), BF16), vm((rows, D), F32), vm((5, RB, D), F32)),
         in_specs=[A] * 14,
-        out_specs=(A,) * 3,
+        out_specs=(V,) * 3,
         scratch_shapes=scratch,
-        compiler_params=pltpu.CompilerParams(vmem_limit_bytes=67043328, collective_id=0, has_side_effects=True),
+        compiler_params=pltpu.CompilerParams(vmem_limit_bytes=LIMIT, collective_id=0, has_side_effects=True),
     )(*args)
     got = pl.pallas_call(
-        functools.partial(finish_kernel, rows),
+        finish_kernel,
         out_shape=outs,
-        in_specs=[A] * 3,
+        in_specs=[V] * 3,
         out_specs=(A,) * 14,
-        scratch_shapes=[vm(o.shape, o.dtype) for o in outs[2:]] + [
-            vm((rows, D), BF16), vm((rows, D), F32), vm((5, RB, D), F32), dma((2, 2, PIECES)), dma((12,)), dma((1,))],
-    )(*got)
+        scratch_shapes=[vm(o.shape, o.dtype) for o in outs[2:]] + [dma((14,))],
+        compiler_params=pltpu.CompilerParams(vmem_limit_bytes=2 * 1024 * 1024),
+    )(*(pltpu.with_memory_space_constraint(v, pltpu.VMEM) for v in got))
     return got[:3] + (got[3].T, got[4], got[5].T) + tuple(got[6:])
 
 

time: 105 us -> 80.1 us (0.76)
  Pallas kernels: 104 us -> 79.1 us
    pallas_call x2, Pallas kernels: 104 us -> 79.1 us  [the longest x1 77.1 us: body(): pl.pallas_call(functools.partial(layer_kernel, cfg), out_shape=(vm((rows,...]
where the time goes in v2:
time: 80.1 us; the launch traced here: 80 us
  Pallas kernels  79.1 us (99%)
  between operations  0.84 us (1%)
    pallas_call x1, Pallas kernels, body(): pl.pallas_call(functools.partial(layer_kernel, cfg), out_shape=(vm((rows,...  77.1 us
    pallas_call x1, Pallas kernels, body(): pl.pallas_call(finish_kernel, out_shape=outs, in_specs=[V] * 3, out_specs...  2.03 us

profile of v2, /device:TPU:0, one launch (start us, length us, event | category | flops | bytes accessed | tf_op | source)
XLA Modules:
  0.0 80.0 jit_solution(16021555667279346108)
XLA Ops:
  0.7 77.1 %shard_map.245 = (bf16[1576,384]{1,0:T(8,128)(2,1)S(1)}, f32[1576,384]{1,0:T(8,128)S(1)}, f32[5,48,384]{2,1,0:T(8,128)S(1)}) custom-call(bf16[1576,384]{1,0:T(8,128)(2,1)} %refs_0_.1, bf16[48,288]{1,0:T(8,128)(2,1)} %refs_1_.1, f32[288]{0:T(512)} %refs_2_.1, bf16[48,96]{1,0:T(8,128)(2,1)} %bitcast.5, f32[384]{0:T(512)} %refs_4_.1, bf16[48,384]{1,0:T(8,128)(2,1)} %refs_5_.1, ...), custom_call_target="tpu_custom_call" | custom-call | tf_op jit(solution)/shard_map/pallas_call | solution.py:746
  77.8 2.0 %shard_map.246 = (bf16[1576,384]{1,0:T(8,128)(2,1)}, f32[1576,384]{1,0:T(8,128)}, f32[48,288]{1,0:T(8,128)}, f32[48,96]{1,0:T(8,128)}, f32[48,384]{1,0:T(8,128)}...) custom-call(bf16[1576,384]{1,0:T(8,128)(2,1)S(1)} %get-tuple-element, ...), custom_call_target="tpu_custom_call" | custom-call | tf_op jit(solution)/shard_map/pallas_call | solution.py:754

commit v3 on v2

--- a/solution.py
+++ b/solution.py
@@ -21,7 +21,7 @@
 BIG = 528
 SMALL = 176
 HC = 512
-LIMIT = 60 * 1024 * 1024
+VMEM = 67_000_000
 
 
 def nn(a, b):
@@ -96,10 +96,10 @@
     o_out, o_grad, small, refs = refs[14], refs[15], refs[16], refs[17:]
     (packed, packed_bias, projection, projection_bias, expansion, expansion_bias, reduction,
      reduction_bias, first_scale, first_shift, second_scale, second_shift,
-     x, up, n1, rows1, qkv, attn, est, rinv, n2, rows2, acc1, rg, act, hg, pgr, inv1, inv2,
+     x, up, n1, rows1, qkv, attn, est, rinv, n2, acc1, act, hg, pgr, inv1,
      wpk, ptr, exr, rtr, wp, pt, exc, rtc, bias,
-     gm, gh, rm1, rm2, rm3, rh1, rh2, rh3, sm1, sm2, sh1, sh2, frame, vec, vsum1, vr1, vr2, vr3, vall,
-     isem, csem, asend, zfirst, zr, pr, kr, bs, gsend, g1r, g2r, g3r, vs) = refs
+     gm, gh, rm1, rm2, rm3, rh1, rh2, rh3, sm1, sm2, sh1, sh2, frame, vec, vq, vr2, vr3,
+     asend, zfirst, pfirst, zr, pr, kr, bs, gsend, g1r, g2r, g3r, glast, vs) = refs
 
     dp_i, col_i = lax.axis_index("dp"), lax.axis_index("col")
     z, pd = dp_i // PD, lax.rem(dp_i, PD)
@@ -120,13 +120,19 @@
         return device(znear(s - 1), pd, y, core)
 
     def pplace(d):
-        q = lax.rem(plane + d, PLANE)
-        return q // Y, lax.rem(q, Y)
+        return lax.rem(pd + d // Y, PD), lax.rem(y + d % Y, Y)
+
+    def psource(d):
+        return lax.rem(pd + PD - d // Y, PD), lax.rem(y + Y - d % Y, Y)
 
     def ppeer(d):
         pp, yy = pplace(d)
         return device(z, pp, yy, core)
 
+    def vpeer(d):
+        pp, yy = pplace(d // 2)
+        return device(z, pp, yy, lax.rem(core + d % 2, 2))
+
     sibling = device(z, pd, y, 1 - core)
 
     def cpeer(d):
@@ -137,17 +143,16 @@
             src_ref=src, dst_ref=dst, send_sem=send, recv_sem=recv, device_id=to, device_id_type=MESH)
 
     barrier = pltpu.get_barrier_semaphore()
-    near = [zpeer(d) for d in range(1, Z)] + [ppeer(d) for d in range(1, PLANE)]
-    near += [cpeer(d) for d in range(1, 2 * Y) if d != Y]
-    for to in near + ([sibling] if Y == 1 else []):
+    near = [zpeer(d) for d in range(1, Z)] + [vpeer(d) for d in range(1, 2 * PLANE)]
+    for to in near:
         pl.semaphore_signal(barrier, inc=1, device_id=to, device_id_type=MESH)
     greeted = len(near)
 
-    cin = pltpu.make_async_copy(tokens, x.at[pl.ds(0, rows)], csem.at[0])
-    cup = pltpu.make_async_copy(upstream, up.at[pl.ds(0, rows)], csem.at[1])
+    cin = pltpu.make_async_copy(tokens, x.at[pl.ds(0, rows)], gsend.at[5])
+    cup = pltpu.make_async_copy(upstream, up.at[pl.ds(0, rows)], gsend.at[6])
     inside = (packed, packed_bias, projection, projection_bias, expansion, expansion_bias, reduction,
               reduction_bias, first_scale, first_shift, second_scale, second_shift)
-    loads = [pltpu.make_async_copy(a, b, isem.at[n]) for n, (a, b) in enumerate(zip(outside, inside))]
+    loads = [pltpu.make_async_copy(a, b, asend.at[n] if n < 8 else gsend.at[n - 8]) for n, (a, b) in enumerate(zip(outside, inside))]
     for n in (0, 2, 4, 6, 1, 5, 3, 7, 8, 9, 10, 11):
         loads[n].start()
     cin.start()
@@ -167,6 +172,74 @@
 
     for h in range(PAIRS):
         wpk[h, z, pd, :, lanes_of(pos, 128)] = frame[:, turn(h)].astype(BF16)
+    chunks = [wpk.at[h] for h in range(PAIRS)] + [ptr]
+    for j in range(FF // HC):
+        chunks += [exr.at[j], rtr.at[j]]
+    mine_l = lanes_of(pos, 128)
+
+    def span(slots):
+        return inv1.at[0:slots * RB // 2]
+
+    def vspan(count):
+        return inv1.at[0:count * 16]
+
+    def arrived(sem, ref):
+        remote(ref, ref, vs.at[0], sem, sibling).wait_recv()
+
+    def left(sem, ref):
+        remote(ref, ref, sem, vs.at[0], sibling).wait_send()
+
+    def zcopy(k, d):
+        slot = chunks[k].at[z, pd, :, mine_l]
+        return remote(slot, slot, asend.at[k], zfirst.at[z] if k == 0 else zr.at[k], zpeer(d))
+
+    def pcopy(k, d):
+        slot = chunks[k].at[:, pd, :, mine_l]
+        return remote(slot, slot, asend.at[k], pr.at[k], ppeer(d))
+
+    def qcopy(d, q):
+        slot = chunks[0].at[q, pd, :, mine_l]
+        return remote(slot, slot, asend.at[0], pfirst.at[d - 1], ppeer(d))
+
+    def scopy(q):
+        slot = chunks[0].at[q, pd, :, mine_l]
+        return remote(slot, slot, asend.at[0], kr.at[0], sibling)
+
+    def scopy_from(d):
+        pp, yy = psource(d)
+        slot = chunks[0].at[:, pp, :, lanes_of(core * Y + yy, 128)]
+        return remote(slot, slot, asend.at[0], kr.at[0], sibling)
+
+    def kcopy(k):
+        slot = chunks[k].at[:, :, :, lanes_of(core, Y * 128)]
+        return remote(slot, slot, asend.at[k], kr.at[k], sibling)
+
+    def bcopy(d):
+        return remote(bias.at[pos], bias.at[pos], bs.at[0], bs.at[1], cpeer(d))
+
+    @named
+    def to_plane(k):
+        arrived(zr.at[k], span(Z - 1))
+        for d in range(1, PLANE):
+            pcopy(k, d).start()
+
+    @named
+    def to_sibling(k):
+        arrived(pr.at[k], span((PLANE - 1) * Z))
+        kcopy(k).start()
+
+    ALL = Z - 1 + (PLANE - 1) * Z + PLANE * Z
+
+    with jax.named_scope("barrier"):
+        pl.semaphore_wait(barrier, greeted)
+    def to_z(k):
+        for d in range(1, Z):
+            zcopy(k, d).start()
+
+    to_z(0)
+    for d in range(1, PLANE):
+        qcopy(d, z).start()
+    scopy(z).start()
     own = padded(projection[...].astype(F32))
     own = jnp.concatenate([own, jnp.zeros((RB, 128 - own.shape[1]), F32)], axis=1)
     ptr[z, pd, :, lanes_of(pos, 128)] = pltpu.roll(own, lax.rem(96 * col_i, 128), 1).astype(BF16)
@@ -177,76 +250,17 @@
     vrow = pltpu.roll(jnp.broadcast_to(vrow, (8, D)), 32 * col_i, 1)
     bias[pos] = jnp.concatenate([vrow[:4], jnp.broadcast_to(expansion_bias[...].reshape(1, -1), (4, D))], axis=0)
 
-    chunks = [wpk.at[h] for h in range(PAIRS)] + [ptr]
-    for j in range(FF // HC):
-        chunks += [exr.at[j], rtr.at[j]]
-    mine_l = lanes_of(pos, 128)
-
-    def span(slots):
-        return inv1.at[0:slots * RB // 2]
-
-    def vspan(count):
-        return n1.at[0:count * 16]
-
-    def arrived(sem, ref):
-        remote(ref, ref, vs.at[0], sem, sibling).wait_recv()
-
-    def left(sem, ref):
-        remote(ref, ref, sem, vs.at[0], sibling).wait_send()
-
-    def zcopy(k, d):
-        slot = chunks[k].at[z, pd, :, mine_l]
-        return remote(slot, slot, asend.at[k], zfirst.at[z] if k == 0 else zr.at[k], zpeer(d))
-
-    def pcopy(k, d):
-        slot = chunks[k].at[:, pd, :, mine_l]
-        return remote(slot, slot, asend.at[k], pr.at[k], ppeer(d))
-
-    def qcopy(d, q):
-        slot = chunks[0].at[q, pd, :, mine_l]
-        return remote(slot, slot, asend.at[0], pr.at[0], ppeer(d))
-
-    def kcopy(k):
-        slot = chunks[k].at[:, :, :, lanes_of(core, Y * 128)]
-        return remote(slot, slot, asend.at[k], kr.at[k], sibling)
-
-    def bcopy(d):
-        return remote(bias.at[pos], bias.at[pos], bs.at[0], bs.at[1], cpeer(d))
-
-    @named
-    def to_plane(k):
-        arrived(zr.at[k], span(Z - 1))
-        for d in range(1, PLANE):
-            pcopy(k, d).start()
-
-    @named
-    def to_sibling(k):
-        arrived(pr.at[k], span((PLANE - 1) * Z))
-        kcopy(k).start()
-
-    ALL = Z - 1 + (PLANE - 1) * Z + PLANE * Z
-
-    with jax.named_scope("barrier"):
-        pl.semaphore_wait(barrier, greeted)
-    def to_z(k):
-        for d in range(1, Z):
-            zcopy(k, d).start()
-
-    to_z(0)
-    for d in range(1, PLANE):
-        qcopy(d, z).start()
     for d in range(1, 2 * Y):
         bcopy(d).start()
 
-    x[rows:, :] = jnp.zeros((RP - rows, D), BF16)
+    x[rows:, :] = jnp.zeros((x.shape[0] - rows, D), BF16)
     up[rows:, :] = jnp.zeros((RP - rows, D), BF16)
     for h in range(PAIRS):
         qkv[h, RP:, :] = jnp.zeros((qkv.shape[1] - RP, D), BF16)
     tail = attn.shape[0] - RP + 16
     attn[RP - 16:, :] = jnp.zeros((tail, D), BF16)
-    act[RP:, :] = jnp.zeros((act.shape[0] - RP, HC), BF16)
     rinv[RP - 16:, :] = jnp.zeros((tail, D), F32)
-    pgr[:, RP - 16:, :] = jnp.zeros((PAIRS, tail, D), BF16)
+    pgr[RP - 16:, :] = jnp.zeros((tail, PAIRS * D), BF16)
     fs = first_scale[...].reshape(1, D)
     fh = first_shift[...].reshape(1, D)
     ss = second_scale[...].reshape(1, D)
@@ -263,7 +277,7 @@
         inv = lax.rsqrt(mean(v * v) - avg * avg + EPS)
         normed = (v - avg) * inv
         n1[s, :] = normed
-        inv1[s, :] = jnp.broadcast_to(inv, (SMALL, 128))
+        inv1[s, 0:64] = jnp.broadcast_to(inv, (SMALL, 64))
         rows1[s, :] = (normed * fs + fh).astype(BF16)
         return 0
 
@@ -273,17 +287,22 @@
         arrived(zfirst.at[q], chunks[0].at[q, pd, :, mine_l])
         for e in range(1, PLANE):
             qcopy(e, q).start()
+        scopy(q).start()
 
     loop(0, nsm, ln1, 0)
-    to_z(1)
+    for k in (1, 2, 3):
+        to_z(k)
     for d in range(1, Z):
         pass_on(d)
-    for k in range(2, len(chunks)):
+    for k in range(4, len(chunks)):
         to_z(k)
-    to_plane(1)
     with jax.named_scope("plane0"):
-        arrived(pr.at[0], span((PLANE - 1) * Z))
-    kcopy(0).start()
+        for d in range(1, PLANE):
+            if d == PLANE - 1:
+                to_plane(1)
+            arrived(pfirst.at[d - 1], span(Z))
+            scopy_from(d).start()
+    to_plane(2)
     arrived(bs.at[1], n1.at[0:8 * (2 * Y - 1)])
 
     lane = lax.broadcasted_iota(jnp.int32, (KEYS, 128), 1)
@@ -321,7 +340,7 @@
     def assemble(h):
         kcopy(h).wait_recv()
         for j, (first, second, upto) in enumerate(TILES[h]):
-            wp[h, :, j * 128:(j + 1) * 128] = merged(
+            wp[:, h * D + j * 128:h * D + (j + 1) * 128] = merged(
                 lambda c: compact(wpk[h, :, :, :, place(c) * 128:(place(c) + 1) * 128]), first, second, upto)
 
     def bias_of(h):
@@ -334,13 +353,23 @@
         last = min(rows, (i + 1) * SMALL)
         ref[i * SMALL:last, :] = value[:last - i * SMALL]
 
+    def again(ref, i):
+        last = min(rows, (i + 1) * SMALL)
+        value = ref[i * SMALL:last, :]
+        more = (i + 1) * SMALL - last
+        return value if not more else jnp.concatenate([value, jnp.zeros((more, D), value.dtype)], axis=0)
+
     def window(i):
         first = i * SEQ
         base = (first // 16) * 16
         return first - base, base if isinstance(i, int) else pl.multiple_of(base, 16)
 
-    before = ((to_sibling, 1), (to_plane, 2)), ((to_sibling, 2),), ((to_sibling, 3),)
-    after = (tuple((to_plane, k) for k in (3, 4, 5, 6)), tuple((to_plane, k) for k in (7, 8, 9)), ((to_sibling, 4), (to_sibling, 5)))
+    before = ((to_plane, 3), (to_plane, 4), (to_sibling, 1)), ((to_plane, 7),), ((to_plane, 9), (to_sibling, 3))
+    after = (
+        ((to_plane, 5), (to_sibling, 2), (to_plane, 6)),
+        ((to_plane, 8),),
+        ((to_sibling, 4),),
+    )
 
     def do(steps):
         for step, k in steps:
@@ -348,15 +377,20 @@
 
     for h in range(PAIRS):
         hl = pl.ds(h * 128, 128)
-        assemble(h)
-        pb = bias_of(h)
-
-        def project(i, _):
-            s = rows_of(i, BIG)
-            qkv[h, s, :] = (nn(rows1[s, :], wp[h]) + pb).astype(BF16)
-            return 0
-
-        loop(0, nbig, project, 0)
+        if h < 2:
+            both = (0,) if h == 0 else tuple(range(1, PAIRS))
+            for g in both:
+                assemble(g)
+            pb = jnp.concatenate([bias_of(g) for g in both], axis=1)
+
+            def project(i, _):
+                s = rows_of(i, BIG)
+                v = (nn(rows1[s, :], wp[:, both[0] * D:(both[-1] + 1) * D]) + pb).astype(BF16)
+                for n, g in enumerate(both):
+                    qkv[g, s, :] = v[:, n * D:(n + 1) * D]
+                return 0
+
+            loop(0, nbig, project, 0)
 
         def attend(i, _):
             off, base = window(i)
@@ -398,7 +432,6 @@
     def exb_of(j):
         return jnp.concatenate([bias[p, 4:5, j * 128:(j + 1) * 128] for p in range(4)], axis=1)
 
-    acc2 = rg
 
     def ln2(i, _):
         s = rows_of(i, SMALL)
@@ -408,11 +441,13 @@
         normed = (v - avg) * inv
         acc1[s, :] = v + rdb
         n2[s, :] = normed
-        inv2[s, :] = jnp.broadcast_to(inv, (SMALL, 128))
-        rows2[s, :] = (normed * ss + sh).astype(BF16)
+        inv1[s, 64:128] = jnp.broadcast_to(inv, (SMALL, 64))
+        x[s, :] = (normed * ss + sh).astype(BF16)
+        keep(o_grad, i, jnp.zeros((SMALL, D), F32))
         return 0
 
     unrolled(0, nsm, ln2, 0)
+    to_sibling(5)
 
     def part(big, small, k):
         return big.at[k] if k < PAIRS else small.at[k - PAIRS]
@@ -440,6 +475,27 @@
         part(sm1, sh1, k)[...] = (own.astype(F32) + part(rm1, rh1, k)[...].astype(F32)).astype(BF16)
         for d in range(1, PLANE):
             g2(k, d).start()
+
+    LAST = 3 + PAIRS
+
+    def piece1(d):
+        pp, yy = pplace(d)
+        return remote(gh.at[PAIRS, :, pp, :, lanes_of((1 - core) * Y + yy, 128)],
+                      rh1.at[PAIRS, :, pp, :, lanes_of(yy, 128)], gsend.at[LAST], glast.at[d], sibling)
+
+    def piece_sum(d):
+        pp, yy = pplace(d)
+        piece1(d).wait_recv()
+        own = gh[PAIRS, :, pp, :, lanes_of(core * Y + yy, 128)]
+        got = rh1[PAIRS, :, pp, :, lanes_of(yy, 128)]
+        sh1[PAIRS, :, pp, :, lanes_of(yy, 128)] = (own.astype(F32) + got.astype(F32)).astype(BF16)
+        if d:
+            g2(LAST, d).start()
+
+    @named
+    def sum1_last(_):
+        for d in list(range(1, PLANE)) + [0]:
+            piece_sum(d)
 
     @named
     def sum2(k):
@@ -465,9 +521,12 @@
         ((to_sibling, 8), (to_sibling, 9), (sum1, 0)),
         ((sum1, 1),),
     )
-    for j in range(FF // HC):
-        for k in (4 + 2 * j, 5 + 2 * j):
-            kcopy(k).wait_recv()
+    NH = FF // HC
+    mlp_in = [((kcopy, 4 + 2 * j), (kcopy, 5 + 2 * j)) for j in range(NH)]
+
+    def chunk(j, _):
+        for n in range(NH):
+            pl.when(j == n)(lambda n=n: (kcopy(4 + 2 * n).wait_recv(), kcopy(5 + 2 * n).wait_recv(), None)[2])
         if RV != RB:
             exc[...] = compact(exr[j])
             rtc[...] = compact(rtr[j])
@@ -478,42 +537,45 @@
         def rt_of():
             return rtc[...] if RV != RB else rtr[j].reshape(D, HC)
 
-        exb = exb_of(j)
-
-        def mlp(i, bsum):
+        tile = lanes_of(j, 128)
+        exb = jnp.concatenate([bias[p, 4:5, tile] for p in range(4)], axis=1)
+        bsum = jnp.zeros((1, HC), F32)
+        for i in range(nbig):
             s = rows_of(i, BIG)
-            pre = nn(rows2[s, :], ex_of()) + exb
+            pre = nn(x[s, :], ex_of()) + exb
             ug = nn(up[s, :], rt_of())
             cdf = 0.5 + 0.5 * lax.erf(pre * ROOT_HALF)
-            act[s, :] = (pre * cdf).astype(BF16)
+            act[j, s, :] = (pre * cdf).astype(BF16)
             g = ug * (cdf + pre * (jnp.exp(pre * pre * -0.5) * INV_ROOT_TAU))
             hg[s, :] = g.astype(BF16)
-            acc1[s, :] += nt(act[s, :], rt_of())
+            last = min(rows, (i + 1) * BIG)
             back = nt(hg[s, :], ex_of())
-            acc2[s, :] = back if j == 0 else acc2[s, :] + back
-            return bsum + jnp.sum(g, axis=0, keepdims=True)
-
-        bsum = loop(0, nbig, mlp, jnp.zeros((1, HC), F32))
-        do(spot[j])
+            o_grad[i * BIG:last, :] += back[:last - i * BIG]
+            bsum += jnp.sum(g, axis=0, keepdims=True)
         for p in range(4):
-            vec[9 + p:10 + p, j * 128:(j + 1) * 128] = bsum[:, p * 128:(p + 1) * 128]
-        for base, g in ((0, tn(rows2[...], hg[...])), (128, tn(up[...], act[0:RP, :]))):
+            vec[9 + p:10 + p, tile] = bsum[:, p * 128:(p + 1) * 128]
+        for n in range(NH):
+            pl.when(j == n)(lambda n=n: do(spot[n]))
+        for base, g in ((0, tn(x[0:RP, :], hg[...])), (128, tn(up[...], act[j]))):
             for p in range(4):
                 gm[j, :, :, :, p * 256 + base:p * 256 + base + 128] = spread(g[:, p * 128:(p + 1) * 128])
-        g1(j).start()
+        for n in range(NH):
+            pl.when(j == n)(lambda n=n: (g1(n).start(), None)[1])
+        return 0
+
+    loop(0, NH, chunk, 0)
 
     def ln2b(i, carry):
         s = rows_of(i, SMALL)
         u = up[s, :].astype(F32)
-        keep(o_out, i, acc1[s, :].astype(BF16))
-        g = acc2[s, :]
+        g = again(o_grad, i)
         normed = n2[s, :]
-        inv = inv2[s, 0:1]
+        inv = inv1[s, 64:65]
         scaled = g * ss
         d = u + inv * (scaled - mean(scaled) - normed * mean(scaled * normed))
-        rg[s, :] = d
+        keep(o_grad, i, d)
         hg[s, 0:D] = d.astype(BF16)
-        act[s, 0:D] = nn(d.astype(BF16), pt[...]).astype(BF16)
+        x[s, :] = nn(d.astype(BF16), pt[...]).astype(BF16)
         terms = (d, u, g * normed, g)
         return tuple(a + jnp.sum(t, axis=0, keepdims=True) for a, t in zip(carry, terms))
 
@@ -555,7 +617,7 @@
             v = qkv[h, kk, 256:384]
             rid = lax.broadcasted_iota(jnp.int32, (WIN, 128), 0) - off
             mine = (rid >= 0) & (rid < SEQ)
-            do = jnp.where(mine, act[qw, hl].astype(F32) * rinv[qw, hl], 0.0)
+            do = jnp.where(mine, x[qw, hl].astype(F32) * rinv[qw, hl], 0.0)
             dob = do.astype(BF16)
             xx = jnp.concatenate([dob, (do * attn[qw, hl].astype(F32)).astype(BF16)], axis=1)
             ev = even[:WIN]
@@ -567,97 +629,113 @@
             dq = (nn(d0, jnp.where(even, k, zero)) + nn(d1, jnp.where(even, zero, k))) * 0.125
             dk = (tn(d0, jnp.where(ev, q, zw)) + tn(d1, jnp.where(ev, zw, q))) * 0.125
             dv = tn(e0, jnp.where(ev, dob, zw)) + tn(e1, jnp.where(ev, zw, dob))
-            old = pgr[h, qw, :].astype(F32)
-            pgr[h, qw, 0:128] = jnp.where(mine, dq, old[:, 0:128]).astype(BF16)
-            pgr[h, qw, 128:256] = jnp.where(mine, dk[:WIN], old[:, 128:256]).astype(BF16)
-            pgr[h, qw, 256:384] = jnp.where(mine, dv[:WIN], old[:, 256:384]).astype(BF16)
+            old = pgr[qw, h * D:(h + 1) * D].astype(F32)
+            pgr[qw, h * D:h * D + 128] = jnp.where(mine, dq, old[:, 0:128]).astype(BF16)
+            pgr[qw, h * D + 128:h * D + 256] = jnp.where(mine, dk[:WIN], old[:, 128:256]).astype(BF16)
+            pgr[qw, h * D + 256:h * D + 384] = jnp.where(mine, dv[:WIN], old[:, 256:384]).astype(BF16)
             return 0
 
         unrolled(0, images, attend_back, 0)
         do(behind[h])
-        gp = tn(rows1[...], pgr[h, 0:RP, :])
+        gp = tn(rows1[...], pgr[0:RP, h * D:(h + 1) * D])
         for c, j in enumerate(SHARES[h]):
             gh[1 + h, :, :, :, place(c) * 128:(place(c) + 1) * 128] = spread(gp[:, j * 128:(j + 1) * 128])
-        g1(4 + h).start()
+        if h < PAIRS - 1:
+            g1(4 + h).start()
+        else:
+            for d in list(range(1, PLANE)) + [0]:
+                piece1(d).start()
 
         def bias_sum(i, carry):
             s = rows_of(i, SMALL)
-            return carry + jnp.sum(pgr[h, s, :].astype(F32), axis=0, keepdims=True)
+            return carry + jnp.sum(pgr[s, h * D:(h + 1) * D].astype(F32), axis=0, keepdims=True)
 
         vec[6 + h:7 + h, :] = unrolled(0, nsm, bias_sum, zr1)
 
-    gbuf = acc1
+    vq[...] = jnp.zeros(vq.shape, F32)
+    for q in range(4):
+        for h in range(PAIRS):
+            j = SHARES[h][q]
+            vq[q, 6 + h:7 + h, :] = vec[6 + h:7 + h, j * 128:(j + 1) * 128]
+            vq[q, 9 + h:10 + h, :] = vec[9 + place(q):10 + place(q), h * 128:(h + 1) * 128]
+
+    gbuf = n2
 
     def ln1b(i, carry):
         s = rows_of(i, SMALL)
-        g = nt(pgr[0, s, :], wp[0]) + nt(pgr[1, s, :], wp[1]) + nt(pgr[2, s, :], wp[2])
+        g = nt(pgr[s, :], wp[...])
         gbuf[s, :] = g
         terms = (g * n1[s, :], g)
-        hook(i, [(nsm // 2, lambda: sum1(6))])
+        hook(i, [(nsm // 2 - 1, lambda: sum1_last(0))])
         return tuple(a + jnp.sum(t, axis=0, keepdims=True) for a, t in zip(carry, terms))
 
     sums = unrolled(0, nsm, ln1b, (zr1,) * 2)
 
     for r, t in zip((2, 3), sums):
         vec[r:r + 1, :] = t
-    def v1():
-        return remote(vec, vr1, vs.at[0], vs.at[1], sibling)
+    wide_d = D // 4
+    for q in range(4):
+        vq[q, 0:6, 0:wide_d] = vec[0:6, q * wide_d:(q + 1) * wide_d]
+    me = plane * 2 + core
 
     def v2(d):
-        return remote(vsum1, vr2.at[plane], vs.at[0], vs.at[2], ppeer(d))
+        to = vpeer(d)
+        return remote(vq.at[to[1]], vr2.at[me], vs.at[0], vs.at[1], to)
 
     def v3(d):
-        return remote(vr3.at[z], vr3.at[z], vs.at[0], vs.at[3], zpeer(d))
-
-    def vector1():
-        v1().wait_recv()
-        vsum1[...] = vec[...] + vr1[...]
-        for d in range(1, PLANE):
-            v2(d).start()
-        vr2[plane] = vsum1[...]
+        return remote(vr3.at[z], vr3.at[z], vs.at[0], vs.at[2], zpeer(d))
 
     def vector2():
-        arrived(vs.at[2], vspan(PLANE - 1))
+        arrived(vs.at[1], vspan(2 * PLANE - 1))
         total = vr2[0]
-        for q in range(1, PLANE):
+        for q in range(1, 2 * PLANE):
             total += vr2[q]
         vr3[z] = total
         for d in range(1, Z):
             v3(d).start()
 
-    v1().start()
+    for d in range(1, 2 * PLANE):
+        v2(d).start()
+    vr2[me] = vq[col_i]
 
     def ln1c(i, _):
         s = rows_of(i, SMALL)
         normed = n1[s, :]
         inv = inv1[s, 0:1]
         scaled = gbuf[s, :] * fs
-        keep(o_grad, i, rg[s, :] + inv * (scaled - mean(scaled) - normed * mean(scaled * normed)))
-        hook(i, [(nsm // 2, vector1)])
+        keep(o_grad, i, again(o_grad, i) + inv * (scaled - mean(scaled) - normed * mean(scaled * normed)))
         return 0
 
     unrolled(0, nsm, ln1c, 0)
-    do(((sum2, 5), (sum2, 6)))
-    with jax.named_scope("vector2"):
-        vector2()
-    do(((finish_mlp, 2), (finish_projection, 3)))
+    def emit(i):
+        s = rows_of(i, BIG)
+        last = min(rows, (i + 1) * BIG)
+        value = acc1[s, :]
+        for j in range(NH):
+            value += nt(act[j, s, :], rtr[j].reshape(D, HC) if RV == RB else compact(rtr[j]))
+        o_out[i * BIG:last, :] = value[:last - i * BIG].astype(BF16)
+
+    with jax.named_scope("emit"):
+        for i in range(nbig):
+            emit(i)
+            do((((sum2, 5), (finish_mlp, 2)), ((finish_projection, 3), (sum2, 6)))[i] if i < 2 else ())
+            if i == min(1, nbig - 1):
+                vector2()
     for h in range(PAIRS - 1):
         frame[:, turn(h)] = sum3(4 + h)
     frame[:, turn(PAIRS - 1)] = sum3(3 + PAIRS)
     back = lax.rem(D - 32 * col_i, D)
     small[0] = pltpu.roll(frame[...], back, 1)
     with jax.named_scope("vec3"):
-        arrived(vs.at[3], vspan(Z - 1))
+        arrived(vs.at[2], vspan(Z - 1))
     total = vr3[0]
     for q in range(1, Z):
         total += vr3[q]
-    vall[...] = total
-    turned = pltpu.roll(total[0:8, :], lax.rem(D - 96 * col_i, D), 1)
-    small[3, 0:8, 128:256] = turned[:, :128]
-    for h, j in enumerate((jnp.minimum(col_i, 2), (col_i + 1) // 2, jnp.maximum(col_i - 1, 0))):
-        frame[0:1, turn(h)] = vall[6 + h:7 + h, lanes_of(j, 128)]
+    small[3, 0:8, 128:256] = total[0:8]
+    for h in range(PAIRS):
+        frame[0:1, turn(h)] = total[6 + h:7 + h]
+        small[4, 8:9, h * 128:(h + 1) * 128] = total[9 + h:10 + h]
     small[4, 0:8, :] = pltpu.roll(frame[0:8, :], back, 1)
-    small[4, 8:9, :] = vall[pl.ds(9 + pos, 1), :]
 
     with jax.named_scope("ends"):
         for k in range(len(chunks)):
@@ -665,7 +743,7 @@
         left(bs.at[0], n1.at[0:8 * (2 * Y - 1)])
         for k in range(7):
             left(gsend.at[k], span(ALL * (width(k) // 128)))
-        left(vs.at[0], vspan(PLANE + Z - 1))
+        left(vs.at[0], vspan(2 * PLANE + Z - 2))
 
 
 def finish_kernel(*refs):
@@ -703,7 +781,9 @@
     RB = -(-RV // 16) * 16
     PLANE = PD * Y
     RP = -(-rows // BIG) * BIG
-    XP = RP + 80
+    reach = ((images - 1) * SEQ) // 16 * 16
+    XQ = max(RP + 16, reach + WIN)
+    XP = max(RP + 16, reach + KEYS)
     cfg = (Z, PD, Y, RB, RV, rows)
     V = pl.BlockSpec(memory_space=pltpu.VMEM)
     A = pl.BlockSpec(memory_space=pl.ANY)
@@ -720,17 +800,16 @@
     ) + (S((D // cols,), F32),) * 5
     narrow = (args[1], args[2], args[3], args[4], args[5], args[6], args[7]) + args[8:13]
     scratch = [vm(a.shape, a.dtype) for a in narrow] + [
-        vm((RP, D), BF16), vm((RP, D), BF16),
+        vm((XQ, D), BF16), vm((RP, D), BF16),
         vm((RP, D), F32), vm((RP, D), BF16),
-        vm((PAIRS, XP, D), BF16), vm((XP, D), BF16),
-        vm((PAIRS, images, 2, WIN, KEYS), BF16), vm((XP, D), F32),
-        vm((RP, D), F32), vm((RP, D), BF16),
+        vm((PAIRS, XP, D), BF16), vm((XQ, D), BF16),
+        vm((PAIRS, images, 2, WIN, KEYS), BF16), vm((XQ, D), F32),
         vm((RP, D), F32), vm((RP, D), F32),
-        vm((XP, HC), BF16), vm((RP, HC), BF16),
-        vm((PAIRS, XP, D), BF16), vm((max(RP, (Z - 1 + (2 * PLANE - 1) * Z) * RB), 128), F32), vm((RP, 128), F32),
+        vm((NH, RP, HC), BF16), vm((RP, HC), BF16),
+        vm((XQ, PAIRS * D), BF16), vm((max(RP, (Z - 1 + (2 * PLANE - 1) * Z) * RB), 128), F32),
         vm((PAIRS, Z, PD, RB, 4 * 128), BF16), vm((Z, PD, RB, 4 * 128), BF16),
         vm((NH, Z, PD, RB, HC), BF16), vm((NH, Z, PD, RB, HC), BF16),
-        vm((PAIRS, D, D), BF16), vm((D, D), BF16),
+        vm((D, PAIRS * D), BF16), vm((D, D), BF16),
         vm((D, HC) if small else (16, 128), BF16), vm((D, HC) if small else (16, 128), BF16),
         vm((4, 8, D), F32),
         vm((NH, Z, PD, RB, 4 * 256), BF16), vm((4, Z, PD, RB, 4 * 128), BF16),
@@ -738,10 +817,10 @@
         vm((4, Z, PD, RB, Y * 128), BF16), vm((4, PLANE - 1, Z, RB, 128), BF16), vm((4, Z, RB, 128), BF16),
         vm((NH, Z, PD, RB, Y * 256), BF16), vm((NH, Z, RB, 256), BF16),
         vm((4, Z, PD, RB, Y * 128), BF16), vm((4, Z, RB, 128), BF16),
-        vm((RB, D), F32), vm((16, D), F32), vm((16, D), F32),
-        vm((16, D), F32), vm((PLANE, 16, D), F32), vm((Z, 16, D), F32), vm((16, D), F32),
-        dma((12,)), dma((2,)), dma((NC,)), dma((Z,)), dma((NC,)), dma((NC,)), dma((NC,)),
-        dma((2,)), dma((7,)), dma((7,)), dma((7,)), dma((7,)), dma((4,)),
+        vm((RB, D), F32), vm((16, D), F32),
+        vm((4, 16, 128), F32), vm((2 * PLANE, 16, 128), F32), vm((Z, 16, 128), F32),
+        dma((NC,)), dma((Z,)), dma((PLANE - 1,)), dma((NC,)), dma((NC,)), dma((NC,)),
+        dma((2,)), dma((7,)), dma((7,)), dma((7,)), dma((7,)), dma((PLANE,)), dma((3,)),
     ]
     got = pl.pallas_call(
         functools.partial(layer_kernel, cfg),
@@ -749,7 +828,7 @@
         in_specs=[A] * 14,
         out_specs=(V,) * 3,
         scratch_shapes=scratch,
-        compiler_params=pltpu.CompilerParams(vmem_limit_bytes=LIMIT, collective_id=0, has_side_effects=True),
+        compiler_params=pltpu.CompilerParams(vmem_limit_bytes=VMEM - rows * D * 6 - 5 * RB * D * 4 - 65536, collective_id=0, has_side_effects=True),
     )(*args)
     got = pl.pallas_call(
         finish_kernel,

time: 80.1 us -> 74.3 us (0.928)
  Pallas kernels: 79.1 us -> 73.3 us
    pallas_call x1, Pallas kernels: 77.1 us -> 71.3 us  [body(): pl.pallas_call(functools.partial(layer_kernel, cfg), out_shape=(vm((rows,...]
where the time goes in v3:
time: 74.3 us; the launch traced here: 74.2 us
  Pallas kernels  73.3 us (99%)
  between operations  0.84 us (1%)
    pallas_call x1, Pallas kernels, body(): pl.pallas_call(functools.partial(layer_kernel, cfg), out_shape=(vm((rows,...  71.3 us
    pallas_call x1, Pallas kernels, body(): pl.pallas_call(finish_kernel, out_shape=outs, in_specs=[V] * 3, out_specs...  2.03 us

profile of v3, /device:TPU:0, one launch (start us, length us, event | category | flops | bytes accessed | tf_op | source)
XLA Modules:
  0.0 74.2 jit_solution(14282067020346297899)
XLA Ops:
  0.7 71.3 %shard_map.245 = (bf16[1576,384]{1,0:T(8,128)(2,1)S(1)}, f32[1576,384]{1,0:T(8,128)S(1)}, f32[5,48,384]{2,1,0:T(8,128)S(1)}) custom-call(bf16[1576,384]{1,0:T(8,128)(2,1)} %refs_0_.1, bf16[48,288]{1,0:T(8,128)(2,1)} %refs_1_.1, f32[288]{0:T(512)} %refs_2_.1, bf16[48,96]{1,0:T(8,128)(2,1)} %bitcast.5, f32[384]{0:T(512)} %refs_4_.1, bf16[48,384]{1,0:T(8,128)(2,1)} %refs_5_.1, ...), custom_call_target="tpu_custom_call" | custom-call | tf_op jit(solution)/shard_map/pallas_call | solution.py:825
  72.0 2.0 %shard_map.246 = (bf16[1576,384]{1,0:T(8,128)(2,1)}, f32[1576,384]{1,0:T(8,128)}, f32[48,288]{1,0:T(8,128)}, f32[48,96]{1,0:T(8,128)}, f32[48,384]{1,0:T(8,128)}...) custom-call(bf16[1576,384]{1,0:T(8,128)(2,1)S(1)} %get-tuple-element, ...), custom_call_target="tpu_custom_call" | custom-call | tf_op jit(solution)/shard_map/pallas_call | solution.py:833

commit v4 on v3

--- a/solution.py
+++ b/solution.py
@@ -157,8 +157,7 @@
         loads[n].start()
     cin.start()
     cup.start()
-    for load in loads:
-        load.wait()
+    loads[0].wait()
 
     def padded(v):
         return v if RV == RB else jnp.concatenate([v, jnp.zeros((RB - RV, v.shape[1]), v.dtype)], axis=0)
@@ -240,6 +239,8 @@
     for d in range(1, PLANE):
         qcopy(d, z).start()
     scopy(z).start()
+    for load in loads[1:]:
+        load.wait()
     own = padded(projection[...].astype(F32))
     own = jnp.concatenate([own, jnp.zeros((RB, 128 - own.shape[1]), F32)], axis=1)
     ptr[z, pd, :, lanes_of(pos, 128)] = pltpu.roll(own, lax.rem(96 * col_i, 128), 1).astype(BF16)
@@ -364,11 +365,11 @@
         base = (first // 16) * 16
         return first - base, base if isinstance(i, int) else pl.multiple_of(base, 16)
 
-    before = ((to_plane, 3), (to_plane, 4), (to_sibling, 1)), ((to_plane, 7),), ((to_plane, 9), (to_sibling, 3))
+    before = ((to_plane, 3), (to_plane, 4), (to_sibling, 1)), ((to_plane, 7),), ((to_plane, 8), (to_plane, 9), (to_sibling, 3), (to_sibling, 4))
     after = (
         ((to_plane, 5), (to_sibling, 2), (to_plane, 6)),
-        ((to_plane, 8),),
-        ((to_sibling, 4),),
+        (),
+        ((to_sibling, 5),),
     )
 
     def do(steps):
@@ -447,7 +448,6 @@
         return 0
 
     unrolled(0, nsm, ln2, 0)
-    to_sibling(5)
 
     def part(big, small, k):
         return big.at[k] if k < PAIRS else small.at[k - PAIRS]
@@ -602,9 +602,10 @@
 
     behind = (
         ((sum1, 3), (sum2, 1)),
-        ((sum1, 4), (sum2, 2), (sum2, 3), (finish_mlp, 0)),
-        ((sum1, 5), (sum2, 4), (finish_mlp, 1)),
+        ((sum1, 4), (sum2, 2)),
+        ((sum1, 5),),
     )
+
     for h in range(PAIRS):
         hl = pl.ds(h * 128, 128)
 
@@ -645,6 +646,7 @@
         else:
             for d in list(range(1, PLANE)) + [0]:
                 piece1(d).start()
+            do(((sum2, 3), (sum2, 4), (finish_mlp, 0), (finish_mlp, 1)))
 
         def bias_sum(i, carry):
             s = rows_of(i, SMALL)
@@ -715,12 +717,15 @@
             value += nt(act[j, s, :], rtr[j].reshape(D, HC) if RV == RB else compact(rtr[j]))
         o_out[i * BIG:last, :] = value[:last - i * BIG].astype(BF16)
 
+    do(((sum2, 5),))
     with jax.named_scope("emit"):
         for i in range(nbig):
             emit(i)
-            do((((sum2, 5), (finish_mlp, 2)), ((finish_projection, 3), (sum2, 6)))[i] if i < 2 else ())
+            if i == 0:
+                do(((sum2, 6),))
             if i == min(1, nbig - 1):
                 vector2()
+        do(((finish_mlp, 2), (finish_projection, 3)))
     for h in range(PAIRS - 1):
         frame[:, turn(h)] = sum3(4 + h)
     frame[:, turn(PAIRS - 1)] = sum3(3 + PAIRS)

time: 74.3 us -> 74 us (level)
  no operation moved by 1% of the time
where the time goes in v4:
time: 74 us; the launch traced here: 73.8 us
  Pallas kernels  73 us (99%)
  between operations  0.84 us (1%)
    pallas_call x1, Pallas kernels, body(): pl.pallas_call(functools.partial(layer_kernel, cfg), out_shape=(vm((rows,...  70.9 us
    pallas_call x1, Pallas kernels, body(): pl.pallas_call(finish_kernel, out_shape=outs, in_specs=[V] * 3, out_specs...  2.03 us

profile of v4, /device:TPU:0, one launch (start us, length us, event | category | flops | bytes accessed | tf_op | source)
XLA Modules:
  0.0 73.8 jit_solution(17152370468730248846)
XLA Ops:
  0.7 70.9 %shard_map.245 = (bf16[1576,384]{1,0:T(8,128)(2,1)S(1)}, f32[1576,384]{1,0:T(8,128)S(1)}, f32[5,48,384]{2,1,0:T(8,128)S(1)}) custom-call(bf16[1576,384]{1,0:T(8,128)(2,1)} %refs_0_.1, bf16[48,288]{1,0:T(8,128)(2,1)} %refs_1_.1, f32[288]{0:T(512)} %refs_2_.1, bf16[48,96]{1,0:T(8,128)(2,1)} %bitcast.5, f32[384]{0:T(512)} %refs_4_.1, bf16[48,384]{1,0:T(8,128)(2,1)} %refs_5_.1, ...), custom_call_target="tpu_custom_call" | custom-call | tf_op jit(solution)/shard_map/pallas_call | solution.py:830
  71.6 2.0 %shard_map.246 = (bf16[1576,384]{1,0:T(8,128)(2,1)}, f32[1576,384]{1,0:T(8,128)}, f32[48,288]{1,0:T(8,128)}, f32[48,96]{1,0:T(8,128)}, f32[48,384]{1,0:T(8,128)}...) custom-call(bf16[1576,384]{1,0:T(8,128)(2,1)S(1)} %get-tuple-element, ...), custom_call_target="tpu_custom_call" | custom-call | tf_op jit(solution)/shard_map/pallas_call | solution.py:838

commit v5 on v4

--- a/solution.py
+++ b/solution.py
@@ -219,7 +219,7 @@
     @named
     def to_plane(k):
         arrived(zr.at[k], span(Z - 1))
-        for d in range(1, PLANE):
+        for d in range(PLANE - 1, 0, -1):
             pcopy(k, d).start()
 
     @named
@@ -232,11 +232,11 @@
     with jax.named_scope("barrier"):
         pl.semaphore_wait(barrier, greeted)
     def to_z(k):
-        for d in range(1, Z):
+        for d in range(Z - 1, 0, -1):
             zcopy(k, d).start()
 
     to_z(0)
-    for d in range(1, PLANE):
+    for d in range(PLANE - 1, 0, -1):
         qcopy(d, z).start()
     scopy(z).start()
     for load in loads[1:]:
@@ -286,7 +286,7 @@
     def pass_on(d):
         q = znear(d - 1)
         arrived(zfirst.at[q], chunks[0].at[q, pd, :, mine_l])
-        for e in range(1, PLANE):
+        for e in range(PLANE - 1, 0, -1):
             qcopy(e, q).start()
         scopy(q).start()
 
@@ -473,7 +473,7 @@
         g1(k).wait_recv()
         own = part(gm, gh, k)[:, :, :, lanes_of(core, Y * width(k))]
         part(sm1, sh1, k)[...] = (own.astype(F32) + part(rm1, rh1, k)[...].astype(F32)).astype(BF16)
-        for d in range(1, PLANE):
+        for d in range(PLANE - 1, 0, -1):
             g2(k, d).start()
 
     LAST = 3 + PAIRS
@@ -494,7 +494,7 @@
 
     @named
     def sum1_last(_):
-        for d in list(range(1, PLANE)) + [0]:
+        for d in range(PLANE - 1, -1, -1):
             piece_sum(d)
 
     @named
@@ -504,7 +504,7 @@
         for d in range(1, PLANE):
             total += part(rm2, rh2, k)[d - 1].astype(F32)
         part(sm2, sh2, k)[...] = total.astype(BF16)
-        for d in range(1, Z):
+        for d in range(Z - 1, 0, -1):
             g3(k, d).start()
 
     @named
@@ -644,16 +644,17 @@
         if h < PAIRS - 1:
             g1(4 + h).start()
         else:
-            for d in list(range(1, PLANE)) + [0]:
+            for d in range(PLANE - 1, -1, -1):
                 piece1(d).start()
             do(((sum2, 3), (sum2, 4), (finish_mlp, 0), (finish_mlp, 1)))
 
-        def bias_sum(i, carry):
-            s = rows_of(i, SMALL)
-            return carry + jnp.sum(pgr[s, h * D:(h + 1) * D].astype(F32), axis=0, keepdims=True)
-
-        vec[6 + h:7 + h, :] = unrolled(0, nsm, bias_sum, zr1)
-
+    def bias_sum(i, carry):
+        s = rows_of(i, SMALL)
+        return carry + jnp.sum(pgr[s, :].astype(F32), axis=0, keepdims=True)
+
+    bsum = unrolled(0, nsm, bias_sum, jnp.zeros((1, PAIRS * D), F32))
+    for h in range(PAIRS):
+        vec[6 + h:7 + h, :] = bsum[:, h * D:(h + 1) * D]
     vq[...] = jnp.zeros(vq.shape, F32)
     for q in range(4):
         for h in range(PAIRS):
@@ -668,7 +669,7 @@
         g = nt(pgr[s, :], wp[...])
         gbuf[s, :] = g
         terms = (g * n1[s, :], g)
-        hook(i, [(nsm // 2 - 1, lambda: sum1_last(0))])
+        hook(i, [(nsm // 2 - 2, lambda: sum1_last(0))])
         return tuple(a + jnp.sum(t, axis=0, keepdims=True) for a, t in zip(carry, terms))
 
     sums = unrolled(0, nsm, ln1b, (zr1,) * 2)
@@ -693,10 +694,10 @@
         for q in range(1, 2 * PLANE):
             total += vr2[q]
         vr3[z] = total
-        for d in range(1, Z):
+        for d in range(Z - 1, 0, -1):
             v3(d).start()
 
-    for d in range(1, 2 * PLANE):
+    for d in range(2 * PLANE - 1, 0, -1):
         v2(d).start()
     vr2[me] = vq[col_i]
 

time: 74 us -> 72.7 us (0.982)
  Pallas kernels: 73 us -> 71.7 us
    pallas_call x1, Pallas kernels: 70.9 us -> 69.7 us  [body(): pl.pallas_call(functools.partial(layer_kernel, cfg), out_shape=(vm((rows,...]
where the time goes in v5:
time: 72.7 us; the launch traced here: 72.6 us
  Pallas kernels  71.7 us (99%)
  between operations  0.84 us (1%)
    pallas_call x1, Pallas kernels, body(): pl.pallas_call(functools.partial(layer_kernel, cfg), out_shape=(vm((rows,...  69.7 us
    pallas_call x1, Pallas kernels, body(): pl.pallas_call(finish_kernel, out_shape=outs, in_specs=[V] * 3, out_specs...  2.03 us

profile of v5, /device:TPU:0, one launch (start us, length us, event | category | flops | bytes accessed | tf_op | source)
XLA Modules:
  0.0 72.6 jit_solution(4970262813997362121)
XLA Ops:
  0.7 69.7 %shard_map.245 = (bf16[1576,384]{1,0:T(8,128)(2,1)S(1)}, f32[1576,384]{1,0:T(8,128)S(1)}, f32[5,48,384]{2,1,0:T(8,128)S(1)}) custom-call(bf16[1576,384]{1,0:T(8,128)(2,1)} %refs_0_.1, bf16[48,288]{1,0:T(8,128)(2,1)} %refs_1_.1, f32[288]{0:T(512)} %refs_2_.1, bf16[48,96]{1,0:T(8,128)(2,1)} %bitcast.5, f32[384]{0:T(512)} %refs_4_.1, bf16[48,384]{1,0:T(8,128)(2,1)} %refs_5_.1, ...), custom_call_target="tpu_custom_call" | custom-call | tf_op jit(solution)/shard_map/pallas_call | solution.py:831
  70.3 2.0 %shard_map.246 = (bf16[1576,384]{1,0:T(8,128)(2,1)}, f32[1576,384]{1,0:T(8,128)}, f32[48,288]{1,0:T(8,128)}, f32[48,96]{1,0:T(8,128)}, f32[48,384]{1,0:T(8,128)}...) custom-call(bf16[1576,384]{1,0:T(8,128)(2,1)S(1)} %get-tuple-element, ...), custom_call_target="tpu_custom_call" | custom-call | tf_op jit(solution)/shard_map/pallas_call | solution.py:839

commit v6 on v5

--- a/solution.py
+++ b/solution.py
@@ -365,9 +365,9 @@
         base = (first // 16) * 16
         return first - base, base if isinstance(i, int) else pl.multiple_of(base, 16)
 
-    before = ((to_plane, 3), (to_plane, 4), (to_sibling, 1)), ((to_plane, 7),), ((to_plane, 8), (to_plane, 9), (to_sibling, 3), (to_sibling, 4))
+    before = ((to_plane, 3),), ((to_plane, 7),), ((to_plane, 8), (to_plane, 9), (to_sibling, 3), (to_sibling, 4))
     after = (
-        ((to_plane, 5), (to_sibling, 2), (to_plane, 6)),
+        ((to_plane, 4), (to_sibling, 1), (to_plane, 5), (to_sibling, 2), (to_plane, 6)),
         (),
         ((to_sibling, 5),),
     )

time: 72.7 us -> 72.2 us (level)
  no operation moved by 1% of the time
where the time goes in v6:
time: 72.2 us; the launch traced here: 72.1 us
  Pallas kernels  71.2 us (99%)
  between operations  0.84 us (1%)
    pallas_call x1, Pallas kernels, body(): pl.pallas_call(functools.partial(layer_kernel, cfg), out_shape=(vm((rows,...  69.2 us
    pallas_call x1, Pallas kernels, body(): pl.pallas_call(finish_kernel, out_shape=outs, in_specs=[V] * 3, out_specs...  2.03 us

profile of v6, /device:TPU:0, one launch (start us, length us, event | category | flops | bytes accessed | tf_op | source)
XLA Modules:
  0.0 72.1 jit_solution(14982028070505989498)
XLA Ops:
  0.7 69.2 %shard_map.245 = (bf16[1576,384]{1,0:T(8,128)(2,1)S(1)}, f32[1576,384]{1,0:T(8,128)S(1)}, f32[5,48,384]{2,1,0:T(8,128)S(1)}) custom-call(bf16[1576,384]{1,0:T(8,128)(2,1)} %refs_0_.1, bf16[48,288]{1,0:T(8,128)(2,1)} %refs_1_.1, f32[288]{0:T(512)} %refs_2_.1, bf16[48,96]{1,0:T(8,128)(2,1)} %bitcast.5, f32[384]{0:T(512)} %refs_4_.1, bf16[48,384]{1,0:T(8,128)(2,1)} %refs_5_.1, ...), custom_call_target="tpu_custom_call" | custom-call | tf_op jit(solution)/shard_map/pallas_call | solution.py:831
  69.9 2.0 %shard_map.246 = (bf16[1576,384]{1,0:T(8,128)(2,1)}, f32[1576,384]{1,0:T(8,128)}, f32[48,288]{1,0:T(8,128)}, f32[48,96]{1,0:T(8,128)}, f32[48,384]{1,0:T(8,128)}...) custom-call(bf16[1576,384]{1,0:T(8,128)(2,1)S(1)} %get-tuple-element, ...), custom_call_target="tpu_custom_call" | custom-call | tf_op jit(solution)/shard_map/pallas_call | solution.py:839
